TPU v7x, 32 devices: a whole 2x2x4 slice. The times are simulated.
32 devices in a mesh: bins: 4 (over x, core), sta: 8 (over z, y).
Axes of the slice: x: 2, y: 2, z: 4, core: 2. Of those that a mesh axis runs over, the one named last changes fastest.
Arguments:
- spectra: bfloat16 [2, 128, 8, 2048], P(None, 'bins', None, 'sta'), may hold values from -110 to 110
- coords: int32 [2, 2048], replicated, may hold values from 0 to 2047
- slowness: int32 [2, 2048], replicated, may hold values from -32 to 31
Outputs:
- beam_power: float32 [128, 2048], P('bins', 'sta')
All inputs are finite; a program needn't handle non-finite values.
Results may differ from a plain program's by a relative error of at most 0.002.
Values may be sent and summed in bfloat16 or wider, within the bound.
No kernel may reach another device: no remote copies, remote signals or barrier semaphores. Data moves between devices by JAX's collectives and lax.ppermute only.
A program may use at most 64 MiB of HBM per device.

v0:
```python
import math

import jax
import jax.numpy as jnp
from jax import lax
from jax.sharding import PartitionSpec as P

phase_modulus = 1048576
two_pi = 2.0 * math.pi
epsilon = 1e-06


def steering_table(delays, bin_number):
    phase_index = jnp.mod(bin_number * delays, phase_modulus)
    phase = phase_index.astype(jnp.float32) * (two_pi / phase_modulus)
    return jnp.concatenate([jnp.cos(phase), jnp.sin(phase)], 0).astype(jnp.bfloat16)


def stack_rows(whitened):
    real_part = whitened[0]
    imag_part = whitened[1]
    upper_rows = jnp.concatenate([real_part, imag_part], 2)
    bottom = jnp.concatenate([imag_part, -real_part], 2)
    return jnp.concatenate([upper_rows, bottom], 1)


def beam_terms(stacked, bin_numbers, coords_part, slow_part):
    row_count = slow_part.shape[1]
    block_size = math.gcd(row_count, 256)
    block_count = row_count // block_size
    groups = jnp.transpose(slow_part.reshape(2, block_count, block_size), (1, 0, 2))

    def one_block(slow_block):
        delays = (
            slow_block[0][None, :] * coords_part[0][:, None]
            + slow_block[1][None, :] * coords_part[1][:, None]
        )

        def one_bin(pair_args):
            bin_rows, bin_number = pair_args
            steering = steering_table(delays, bin_number)
            return lax.dot_general(
                steering, bin_rows, (((0,), (1,)), ((), ())), preferred_element_type=jnp.float32
            )

        amps = lax.map(one_bin, (stacked, bin_numbers))
        return jnp.transpose(amps, (1, 0, 2)).reshape(block_size, -1)

    blocks = lax.map(one_block, groups)
    return blocks.reshape(row_count, -1)


def local(spectra, coords, slowness):
    bins_dev = spectra.shape[1]
    seg_count = spectra.shape[2]
    values = spectra.astype(jnp.float32)
    local_sq = jnp.sum(values * values, axis=(0, 1))
    total_bins = bins_dev * lax.axis_size("bins")
    totals = lax.psum(local_sq, "bins")
    scale = jnp.sqrt(totals / (2 * total_bins) + epsilon)
    whitened = (values / scale).astype(jnp.bfloat16)
    bin_numbers = lax.axis_index("bins") * bins_dev + 1 + jnp.arange(bins_dev, dtype=jnp.int32)
    stations = coords.shape[1]
    beam_count = slowness.shape[1]
    beams_dev = beam_count // lax.axis_size("sta")
    own_index = lax.axis_index("sta")
    own_beams = lax.dynamic_slice_in_dim(slowness, own_index * beams_dev, beams_dev, 1)
    amplitude = beam_terms(
        stack_rows(lax.all_gather(whitened, "sta", axis=3, tiled=True)),
        bin_numbers,
        coords,
        own_beams,
    )
    amplitude = amplitude.reshape(beams_dev, bins_dev, 2 * seg_count)
    beam_power = jnp.sum(amplitude * amplitude, axis=2).T / (stations * seg_count)
    return beam_power


def solution(mesh):
    in_specs = (P(None, "bins", None, "sta"), P(), P())
    out_specs = P("bins", "sta")
    return jax.shard_map(local, mesh=mesh, in_specs=in_specs, out_specs=out_specs, check_vma=False)
```

profile of v0, /device:TPU:0, one launch (start us, length us, event | category | flops | bytes accessed | tf_op | source)
XLA Modules:
  0.0 470.2 jit_solution(747658920885692020)
XLA Ops:
  7.6 8.5 %psum.7 = f32[8,256]{1,0:T(8,128)S(1)} all-reduce(f32[8,256]{1,0:T(8,128)S(1)} %fusion.19), channel_id=1, replica_groups=mesh['bins'=4,'sta'=8] {'bins'}, use_global_device_ids=true, to_apply=%region_1.0 | all-reduce | flops 2048 | bytes 16384 | tf_op jit(solution)/shard_map/psum | solution.py:59
  16.1 1.7 fusion.20
  19.6 49.1 %all-gather.2.cloned.1.call-done = bf16[2,32,8,2048]{3,2,1,0:T(8,128)(2,1)} async-done(((bf16[2,32,8,256]{3,2,1,0:T(8,128)(2,1)}), bf16[2,32,8,2048]{3,2,1,0:T(8,128)(2,1)}) %all-gather.2.cloned.1.call-update) | async-done | bytes 2097168 | tf_op jit(solution)/shard_map/all_gather | solution.py:69
  68.7 1.9 slice_bitcast_fusion.1
  71.0 2.2 maximum_maximum_fusion
  73.2 389.5 %while.20 = (s32[]{:T(128)}, f32[32,256,16]{1,2,0:T(8,128)S(1)}, s32[32]{0:T(128)S(1)}, bf16[32,16,4096]{2,1,0:T(8,128)(2,1)}, s32[2048]{0:T(1024)S(1)}, /*index...) while((s32[]{:T(128)}, f32[32,256,16]{1,2,0:T(8,128)S(1)}, s32[32]{0:T(128)S(1)}, ...), condition=%wide.region_3.4_spmd.clone, body=%wide.region_2.3_spmd.clone.sunk | while | flops 47710208 | bytes 4361325 | solution.py:46
  73.8 10.3 %cosine_convert_fusion.2 = (bf16[2048,256]{1,0:T(8,128)(2,1)S(1)}, bf16[2048,256]{1,0:T(8,128)(2,1)S(1)}) fusion(s32[2048]{0:T(1024)S(1)} %get-tuple-element.213, s32[256]{0:T(256)S(1)} %get-tuple-element.214, s32[2048]{0:T(1024)S(1)} %get-tuple-element.211, s32[256]{0:T(256)S(1)} %get-tuple-element.212, s32[]{:T(128)} %bitcast.23), kind=kLoop, calls=%fused_computation.13.clone.1 | loop fusion | flops 9961472 | bytes 2115588 | tf_op jit(solution)/shard_map/convert
  84.1 1.3 fusion.29
  86.0 10.3 %cosine_convert_fusion.2 = (bf16[2048,256]{1,0:T(8,128)(2,1)S(1)}, bf16[2048,256]{1,0:T(8,128)(2,1)S(1)}) fusion(s32[2048]{0:T(1024)S(1)} %get-tuple-element.213, s32[256]{0:T(256)S(1)} %get-tuple-element.214, s32[2048]{0:T(1024)S(1)} %get-tuple-element.211, s32[256]{0:T(256)S(1)} %get-tuple-element.212, s32[]{:T(128)} %bitcast.23), kind=kLoop, calls=%fused_computation.13.clone.1 | loop fusion | flops 9961472 | bytes 2115588 | tf_op jit(solution)/shard_map/convert
  96.2 1.3 fusion.29
  98.1 10.3 %cosine_convert_fusion.2 = (bf16[2048,256]{1,0:T(8,128)(2,1)S(1)}, bf16[2048,256]{1,0:T(8,128)(2,1)S(1)}) fusion(s32[2048]{0:T(1024)S(1)} %get-tuple-element.213, s32[256]{0:T(256)S(1)} %get-tuple-element.214, s32[2048]{0:T(1024)S(1)} %get-tuple-element.211, s32[256]{0:T(256)S(1)} %get-tuple-element.212, s32[]{:T(128)} %bitcast.23), kind=kLoop, calls=%fused_computation.13.clone.1 | loop fusion | flops 9961472 | bytes 2115588 | tf_op jit(solution)/shard_map/convert
  108.4 1.3 fusion.29
  110.3 10.3 %cosine_convert_fusion.2 = (bf16[2048,256]{1,0:T(8,128)(2,1)S(1)}, bf16[2048,256]{1,0:T(8,128)(2,1)S(1)}) fusion(s32[2048]{0:T(1024)S(1)} %get-tuple-element.213, s32[256]{0:T(256)S(1)} %get-tuple-element.214, s32[2048]{0:T(1024)S(1)} %get-tuple-element.211, s32[256]{0:T(256)S(1)} %get-tuple-element.212, s32[]{:T(128)} %bitcast.23), kind=kLoop, calls=%fused_computation.13.clone.1 | loop fusion | flops 9961472 | bytes 2115588 | tf_op jit(solution)/shard_map/convert
  120.6 1.3 fusion.29
  122.5 10.3 %cosine_convert_fusion.2 = (bf16[2048,256]{1,0:T(8,128)(2,1)S(1)}, bf16[2048,256]{1,0:T(8,128)(2,1)S(1)}) fusion(s32[2048]{0:T(1024)S(1)} %get-tuple-element.213, s32[256]{0:T(256)S(1)} %get-tuple-element.214, s32[2048]{0:T(1024)S(1)} %get-tuple-element.211, s32[256]{0:T(256)S(1)} %get-tuple-element.212, s32[]{:T(128)} %bitcast.23), kind=kLoop, calls=%fused_computation.13.clone.1 | loop fusion | flops 9961472 | bytes 2115588 | tf_op jit(solution)/shard_map/convert
  132.7 1.3 fusion.29
  134.7 10.3 %cosine_convert_fusion.2 = (bf16[2048,256]{1,0:T(8,128)(2,1)S(1)}, bf16[2048,256]{1,0:T(8,128)(2,1)S(1)}) fusion(s32[2048]{0:T(1024)S(1)} %get-tuple-element.213, s32[256]{0:T(256)S(1)} %get-tuple-element.214, s32[2048]{0:T(1024)S(1)} %get-tuple-element.211, s32[256]{0:T(256)S(1)} %get-tuple-element.212, s32[]{:T(128)} %bitcast.23), kind=kLoop, calls=%fused_computation.13.clone.1 | loop fusion | flops 9961472 | bytes 2115588 | tf_op jit(solution)/shard_map/convert
  144.9 1.3 fusion.29
  146.8 10.3 %cosine_convert_fusion.2 = (bf16[2048,256]{1,0:T(8,128)(2,1)S(1)}, bf16[2048,256]{1,0:T(8,128)(2,1)S(1)}) fusion(s32[2048]{0:T(1024)S(1)} %get-tuple-element.213, s32[256]{0:T(256)S(1)} %get-tuple-element.214, s32[2048]{0:T(1024)S(1)} %get-tuple-element.211, s32[256]{0:T(256)S(1)} %get-tuple-element.212, s32[]{:T(128)} %bitcast.23), kind=kLoop, calls=%fused_computation.13.clone.1 | loop fusion | flops 9961472 | bytes 2115588 | tf_op jit(solution)/shard_map/convert
  157.1 1.3 fusion.29
  159.0 10.3 %cosine_convert_fusion.2 = (bf16[2048,256]{1,0:T(8,128)(2,1)S(1)}, bf16[2048,256]{1,0:T(8,128)(2,1)S(1)}) fusion(s32[2048]{0:T(1024)S(1)} %get-tuple-element.213, s32[256]{0:T(256)S(1)} %get-tuple-element.214, s32[2048]{0:T(1024)S(1)} %get-tuple-element.211, s32[256]{0:T(256)S(1)} %get-tuple-element.212, s32[]{:T(128)} %bitcast.23), kind=kLoop, calls=%fused_computation.13.clone.1 | loop fusion | flops 9961472 | bytes 2115588 | tf_op jit(solution)/shard_map/convert
  169.3 1.3 fusion.29
  171.2 10.3 %cosine_convert_fusion.2 = (bf16[2048,256]{1,0:T(8,128)(2,1)S(1)}, bf16[2048,256]{1,0:T(8,128)(2,1)S(1)}) fusion(s32[2048]{0:T(1024)S(1)} %get-tuple-element.213, s32[256]{0:T(256)S(1)} %get-tuple-element.214, s32[2048]{0:T(1024)S(1)} %get-tuple-element.211, s32[256]{0:T(256)S(1)} %get-tuple-element.212, s32[]{:T(128)} %bitcast.23), kind=kLoop, calls=%fused_computation.13.clone.1 | loop fusion | flops 9961472 | bytes 2115588 | tf_op jit(solution)/shard_map/convert
  181.4 1.3 fusion.29
  183.3 10.3 %cosine_convert_fusion.2 = (bf16[2048,256]{1,0:T(8,128)(2,1)S(1)}, bf16[2048,256]{1,0:T(8,128)(2,1)S(1)}) fusion(s32[2048]{0:T(1024)S(1)} %get-tuple-element.213, s32[256]{0:T(256)S(1)} %get-tuple-element.214, s32[2048]{0:T(1024)S(1)} %get-tuple-element.211, s32[256]{0:T(256)S(1)} %get-tuple-element.212, s32[]{:T(128)} %bitcast.23), kind=kLoop, calls=%fused_computation.13.clone.1 | loop fusion | flops 9961472 | bytes 2115588 | tf_op jit(solution)/shard_map/convert
  193.6 1.3 fusion.29
  195.5 10.3 %cosine_convert_fusion.2 = (bf16[2048,256]{1,0:T(8,128)(2,1)S(1)}, bf16[2048,256]{1,0:T(8,128)(2,1)S(1)}) fusion(s32[2048]{0:T(1024)S(1)} %get-tuple-element.213, s32[256]{0:T(256)S(1)} %get-tuple-element.214, s32[2048]{0:T(1024)S(1)} %get-tuple-element.211, s32[256]{0:T(256)S(1)} %get-tuple-element.212, s32[]{:T(128)} %bitcast.23), kind=kLoop, calls=%fused_computation.13.clone.1 | loop fusion | flops 9961472 | bytes 2115588 | tf_op jit(solution)/shard_map/convert
  205.8 1.3 fusion.29
  207.7 10.3 %cosine_convert_fusion.2 = (bf16[2048,256]{1,0:T(8,128)(2,1)S(1)}, bf16[2048,256]{1,0:T(8,128)(2,1)S(1)}) fusion(s32[2048]{0:T(1024)S(1)} %get-tuple-element.213, s32[256]{0:T(256)S(1)} %get-tuple-element.214, s32[2048]{0:T(1024)S(1)} %get-tuple-element.211, s32[256]{0:T(256)S(1)} %get-tuple-element.212, s32[]{:T(128)} %bitcast.23), kind=kLoop, calls=%fused_computation.13.clone.1 | loop fusion | flops 9961472 | bytes 2115588 | tf_op jit(solution)/shard_map/convert
  217.9 1.3 fusion.29
  219.9 10.3 %cosine_convert_fusion.2 = (bf16[2048,256]{1,0:T(8,128)(2,1)S(1)}, bf16[2048,256]{1,0:T(8,128)(2,1)S(1)}) fusion(s32[2048]{0:T(1024)S(1)} %get-tuple-element.213, s32[256]{0:T(256)S(1)} %get-tuple-element.214, s32[2048]{0:T(1024)S(1)} %get-tuple-element.211, s32[256]{0:T(256)S(1)} %get-tuple-element.212, s32[]{:T(128)} %bitcast.23), kind=kLoop, calls=%fused_computation.13.clone.1 | loop fusion | flops 9961472 | bytes 2115588 | tf_op jit(solution)/shard_map/convert
  230.1 1.3 fusion.29
  232.0 10.3 %cosine_convert_fusion.2 = (bf16[2048,256]{1,0:T(8,128)(2,1)S(1)}, bf16[2048,256]{1,0:T(8,128)(2,1)S(1)}) fusion(s32[2048]{0:T(1024)S(1)} %get-tuple-element.213, s32[256]{0:T(256)S(1)} %get-tuple-element.214, s32[2048]{0:T(1024)S(1)} %get-tuple-element.211, s32[256]{0:T(256)S(1)} %get-tuple-element.212, s32[]{:T(128)} %bitcast.23), kind=kLoop, calls=%fused_computation.13.clone.1 | loop fusion | flops 9961472 | bytes 2115588 | tf_op jit(solution)/shard_map/convert
  244.2 10.3 %cosine_convert_fusion.2 = (bf16[2048,256]{1,0:T(8,128)(2,1)S(1)}, bf16[2048,256]{1,0:T(8,128)(2,1)S(1)}) fusion(s32[2048]{0:T(1024)S(1)} %get-tuple-element.213, s32[256]{0:T(256)S(1)} %get-tuple-element.214, s32[2048]{0:T(1024)S(1)} %get-tuple-element.211, s32[256]{0:T(256)S(1)} %get-tuple-element.212, s32[]{:T(128)} %bitcast.23), kind=kLoop, calls=%fused_computation.13.clone.1 | loop fusion | flops 9961472 | bytes 2115588 | tf_op jit(solution)/shard_map/convert
  256.4 10.3 %cosine_convert_fusion.2 = (bf16[2048,256]{1,0:T(8,128)(2,1)S(1)}, bf16[2048,256]{1,0:T(8,128)(2,1)S(1)}) fusion(s32[2048]{0:T(1024)S(1)} %get-tuple-element.213, s32[256]{0:T(256)S(1)} %get-tuple-element.214, s32[2048]{0:T(1024)S(1)} %get-tuple-element.211, s32[256]{0:T(256)S(1)} %get-tuple-element.212, s32[]{:T(128)} %bitcast.23), kind=kLoop, calls=%fused_computation.13.clone.1 | loop fusion | flops 9961472 | bytes 2115588 | tf_op jit(solution)/shard_map/convert
  266.6 1.3 fusion.29
  268.5 10.3 %cosine_convert_fusion.2 = (bf16[2048,256]{1,0:T(8,128)(2,1)S(1)}, bf16[2048,256]{1,0:T(8,128)(2,1)S(1)}) fusion(s32[2048]{0:T(1024)S(1)} %get-tuple-element.213, s32[256]{0:T(256)S(1)} %get-tuple-element.214, s32[2048]{0:T(1024)S(1)} %get-tuple-element.211, s32[256]{0:T(256)S(1)} %get-tuple-element.212, s32[]{:T(128)} %bitcast.23), kind=kLoop, calls=%fused_computation.13.clone.1 | loop fusion | flops 9961472 | bytes 2115588 | tf_op jit(solution)/shard_map/convert
  278.8 1.3 fusion.29
  280.7 10.3 %cosine_convert_fusion.2 = (bf16[2048,256]{1,0:T(8,128)(2,1)S(1)}, bf16[2048,256]{1,0:T(8,128)(2,1)S(1)}) fusion(s32[2048]{0:T(1024)S(1)} %get-tuple-element.213, s32[256]{0:T(256)S(1)} %get-tuple-element.214, s32[2048]{0:T(1024)S(1)} %get-tuple-element.211, s32[256]{0:T(256)S(1)} %get-tuple-element.212, s32[]{:T(128)} %bitcast.23), kind=kLoop, calls=%fused_computation.13.clone.1 | loop fusion | flops 9961472 | bytes 2115588 | tf_op jit(solution)/shard_map/convert
  291.0 1.3 fusion.29
  292.9 10.3 %cosine_convert_fusion.2 = (bf16[2048,256]{1,0:T(8,128)(2,1)S(1)}, bf16[2048,256]{1,0:T(8,128)(2,1)S(1)}) fusion(s32[2048]{0:T(1024)S(1)} %get-tuple-element.213, s32[256]{0:T(256)S(1)} %get-tuple-element.214, s32[2048]{0:T(1024)S(1)} %get-tuple-element.211, s32[256]{0:T(256)S(1)} %get-tuple-element.212, s32[]{:T(128)} %bitcast.23), kind=kLoop, calls=%fused_computation.13.clone.1 | loop fusion | flops 9961472 | bytes 2115588 | tf_op jit(solution)/shard_map/convert
  303.1 1.3 fusion.29
  305.1 10.3 %cosine_convert_fusion.2 = (bf16[2048,256]{1,0:T(8,128)(2,1)S(1)}, bf16[2048,256]{1,0:T(8,128)(2,1)S(1)}) fusion(s32[2048]{0:T(1024)S(1)} %get-tuple-element.213, s32[256]{0:T(256)S(1)} %get-tuple-element.214, s32[2048]{0:T(1024)S(1)} %get-tuple-element.211, s32[256]{0:T(256)S(1)} %get-tuple-element.212, s32[]{:T(128)} %bitcast.23), kind=kLoop, calls=%fused_computation.13.clone.1 | loop fusion | flops 9961472 | bytes 2115588 | tf_op jit(solution)/shard_map/convert
  315.3 1.3 fusion.29
  317.2 10.3 %cosine_convert_fusion.2 = (bf16[2048,256]{1,0:T(8,128)(2,1)S(1)}, bf16[2048,256]{1,0:T(8,128)(2,1)S(1)}) fusion(s32[2048]{0:T(1024)S(1)} %get-tuple-element.213, s32[256]{0:T(256)S(1)} %get-tuple-element.214, s32[2048]{0:T(1024)S(1)} %get-tuple-element.211, s32[256]{0:T(256)S(1)} %get-tuple-element.212, s32[]{:T(128)} %bitcast.23), kind=kLoop, calls=%fused_computation.13.clone.1 | loop fusion | flops 9961472 | bytes 2115588 | tf_op jit(solution)/shard_map/convert
  327.5 1.3 fusion.29
  329.4 10.3 %cosine_convert_fusion.2 = (bf16[2048,256]{1,0:T(8,128)(2,1)S(1)}, bf16[2048,256]{1,0:T(8,128)(2,1)S(1)}) fusion(s32[2048]{0:T(1024)S(1)} %get-tuple-element.213, s32[256]{0:T(256)S(1)} %get-tuple-element.214, s32[2048]{0:T(1024)S(1)} %get-tuple-element.211, s32[256]{0:T(256)S(1)} %get-tuple-element.212, s32[]{:T(128)} %bitcast.23), kind=kLoop, calls=%fused_computation.13.clone.1 | loop fusion | flops 9961472 | bytes 2115588 | tf_op jit(solution)/shard_map/convert
  339.7 1.3 fusion.29
  341.6 10.3 %cosine_convert_fusion.2 = (bf16[2048,256]{1,0:T(8,128)(2,1)S(1)}, bf16[2048,256]{1,0:T(8,128)(2,1)S(1)}) fusion(s32[2048]{0:T(1024)S(1)} %get-tuple-element.213, s32[256]{0:T(256)S(1)} %get-tuple-element.214, s32[2048]{0:T(1024)S(1)} %get-tuple-element.211, s32[256]{0:T(256)S(1)} %get-tuple-element.212, s32[]{:T(128)} %bitcast.23), kind=kLoop, calls=%fused_computation.13.clone.1 | loop fusion | flops 9961472 | bytes 2115588 | tf_op jit(solution)/shard_map/convert
  351.8 1.3 fusion.29
  353.7 10.3 %cosine_convert_fusion.2 = (bf16[2048,256]{1,0:T(8,128)(2,1)S(1)}, bf16[2048,256]{1,0:T(8,128)(2,1)S(1)}) fusion(s32[2048]{0:T(1024)S(1)} %get-tuple-element.213, s32[256]{0:T(256)S(1)} %get-tuple-element.214, s32[2048]{0:T(1024)S(1)} %get-tuple-element.211, s32[256]{0:T(256)S(1)} %get-tuple-element.212, s32[]{:T(128)} %bitcast.23), kind=kLoop, calls=%fused_computation.13.clone.1 | loop fusion | flops 9961472 | bytes 2115588 | tf_op jit(solution)/shard_map/convert
  364.0 1.3 fusion.29
  365.9 10.3 %cosine_convert_fusion.2 = (bf16[2048,256]{1,0:T(8,128)(2,1)S(1)}, bf16[2048,256]{1,0:T(8,128)(2,1)S(1)}) fusion(s32[2048]{0:T(1024)S(1)} %get-tuple-element.213, s32[256]{0:T(256)S(1)} %get-tuple-element.214, s32[2048]{0:T(1024)S(1)} %get-tuple-element.211, s32[256]{0:T(256)S(1)} %get-tuple-element.212, s32[]{:T(128)} %bitcast.23), kind=kLoop, calls=%fused_computation.13.clone.1 | loop fusion | flops 9961472 | bytes 2115588 | tf_op jit(solution)/shard_map/convert
  376.2 1.3 fusion.29
  378.1 10.3 %cosine_convert_fusion.2 = (bf16[2048,256]{1,0:T(8,128)(2,1)S(1)}, bf16[2048,256]{1,0:T(8,128)(2,1)S(1)}) fusion(s32[2048]{0:T(1024)S(1)} %get-tuple-element.213, s32[256]{0:T(256)S(1)} %get-tuple-element.214, s32[2048]{0:T(1024)S(1)} %get-tuple-element.211, s32[256]{0:T(256)S(1)} %get-tuple-element.212, s32[]{:T(128)} %bitcast.23), kind=kLoop, calls=%fused_computation.13.clone.1 | loop fusion | flops 9961472 | bytes 2115588 | tf_op jit(solution)/shard_map/convert
  388.3 1.3 fusion.29
  390.3 10.3 %cosine_convert_fusion.2 = (bf16[2048,256]{1,0:T(8,128)(2,1)S(1)}, bf16[2048,256]{1,0:T(8,128)(2,1)S(1)}) fusion(s32[2048]{0:T(1024)S(1)} %get-tuple-element.213, s32[256]{0:T(256)S(1)} %get-tuple-element.214, s32[2048]{0:T(1024)S(1)} %get-tuple-element.211, s32[256]{0:T(256)S(1)} %get-tuple-element.212, s32[]{:T(128)} %bitcast.23), kind=kLoop, calls=%fused_computation.13.clone.1 | loop fusion | flops 9961472 | bytes 2115588 | tf_op jit(solution)/shard_map/convert
  400.5 1.3 fusion.29
  402.4 10.3 %cosine_convert_fusion.2 = (bf16[2048,256]{1,0:T(8,128)(2,1)S(1)}, bf16[2048,256]{1,0:T(8,128)(2,1)S(1)}) fusion(s32[2048]{0:T(1024)S(1)} %get-tuple-element.213, s32[256]{0:T(256)S(1)} %get-tuple-element.214, s32[2048]{0:T(1024)S(1)} %get-tuple-element.211, s32[256]{0:T(256)S(1)} %get-tuple-element.212, s32[]{:T(128)} %bitcast.23), kind=kLoop, calls=%fused_computation.13.clone.1 | loop fusion | flops 9961472 | bytes 2115588 | tf_op jit(solution)/shard_map/convert
  412.7 1.3 fusion.29
  414.6 10.3 %cosine_convert_fusion.2 = (bf16[2048,256]{1,0:T(8,128)(2,1)S(1)}, bf16[2048,256]{1,0:T(8,128)(2,1)S(1)}) fusion(s32[2048]{0:T(1024)S(1)} %get-tuple-element.213, s32[256]{0:T(256)S(1)} %get-tuple-element.214, s32[2048]{0:T(1024)S(1)} %get-tuple-element.211, s32[256]{0:T(256)S(1)} %get-tuple-element.212, s32[]{:T(128)} %bitcast.23), kind=kLoop, calls=%fused_computation.13.clone.1 | loop fusion | flops 9961472 | bytes 2115588 | tf_op jit(solution)/shard_map/convert
  426.8 10.3 %cosine_convert_fusion.2 = (bf16[2048,256]{1,0:T(8,128)(2,1)S(1)}, bf16[2048,256]{1,0:T(8,128)(2,1)S(1)}) fusion(s32[2048]{0:T(1024)S(1)} %get-tuple-element.213, s32[256]{0:T(256)S(1)} %get-tuple-element.214, s32[2048]{0:T(1024)S(1)} %get-tuple-element.211, s32[256]{0:T(256)S(1)} %get-tuple-element.212, s32[]{:T(128)} %bitcast.23), kind=kLoop, calls=%fused_computation.13.clone.1 | loop fusion | flops 9961472 | bytes 2115588 | tf_op jit(solution)/shard_map/convert
  438.9 10.3 %cosine_convert_fusion.2 = (bf16[2048,256]{1,0:T(8,128)(2,1)S(1)}, bf16[2048,256]{1,0:T(8,128)(2,1)S(1)}) fusion(s32[2048]{0:T(1024)S(1)} %get-tuple-element.213, s32[256]{0:T(256)S(1)} %get-tuple-element.214, s32[2048]{0:T(1024)S(1)} %get-tuple-element.211, s32[256]{0:T(256)S(1)} %get-tuple-element.212, s32[]{:T(128)} %bitcast.23), kind=kLoop, calls=%fused_computation.13.clone.1 | loop fusion | flops 9961472 | bytes 2115588 | tf_op jit(solution)/shard_map/convert
  451.1 10.3 %cosine_convert_fusion.2 = (bf16[2048,256]{1,0:T(8,128)(2,1)S(1)}, bf16[2048,256]{1,0:T(8,128)(2,1)S(1)}) fusion(s32[2048]{0:T(1024)S(1)} %get-tuple-element.213, s32[256]{0:T(256)S(1)} %get-tuple-element.214, s32[2048]{0:T(1024)S(1)} %get-tuple-element.211, s32[256]{0:T(256)S(1)} %get-tuple-element.212, s32[]{:T(128)} %bitcast.23), kind=kLoop, calls=%fused_computation.13.clone.1 | loop fusion | flops 9961472 | bytes 2115588 | tf_op jit(solution)/shard_map/convert
  (51 shorter events, 31.4 us)
Async XLA Ops:
  6.5 62.2 %all-gather.2.cloned.1.call-start = ((), (), s32[]{:S(2)}) async-start(), calls=%async_computation | async-start | bytes 2359296 | tf_op jit(solution)/shard_map/all_gather | solution.py:69
  68.7 2.2 copy-start
Sparse Core Ops, SparseCore 0:
  18.0 50.6 all-gather.1
where the time goes:
time: 471 us; the launch traced here: 470 us
  other arithmetic  334 us (71%)
  waiting for transfers between devices  49.2 us (10%)
  matrix products  41.3 us (9%)
  local copies, waits for them, and re-layouts  23.8 us (5%)
  between operations  13.5 us (3%)
  blocking collectives  8.52 us (2%)
    another operation x33, other arithmetic  328 us
    all_gather x1, waiting for transfers between devices, local(): lax.all_gather(whitened, 'sta', axis=3, tiled=True)  49.1 us
    dot_general x32, matrix products, one_bin(): lax.dot_general(steering, bin_rows, (((0,), (1,)), ((), ())), preferred_e...  41.3 us
    dynamic_slice x32, local copies, waits for them, and re-layouts, one_block(): amps = lax.map(one_bin, (stacked, bin_numbers))  19.9 us
  transfers between devices with their start and end apart: 1, of which 1 were waited for; matrix products, arithmetic and copies ran while one was open for 0% of the time, Pallas kernels for 0%

commit v1 on v0

v1 whole, which is shorter than its diff:
```python
import functools
import math

import jax
import jax.numpy as jnp
from jax import lax
from jax.experimental import pallas as pl
from jax.experimental.pallas import tpu as pltpu
from jax.sharding import PartitionSpec as P

phase_modulus = 1048576
two_pi = 2.0 * math.pi
epsilon = 1e-06
grid_low = -32
grid_size = 64
lane = 128


def cos_sin(index):
    quarter = phase_modulus // 4
    shift = quarter.bit_length() - 1
    turn = (index + quarter // 2) >> shift
    rest = index - (turn << shift)
    x = rest.astype(jnp.float32) * (two_pi / phase_modulus)
    y = x * x
    s = x + x * y * (-1 / 6 + y * (1 / 120 + y * (-1 / 5040 + y * (1 / 362880))))
    c = 1 + y * (-1 / 2 + y * (1 / 24 + y * (-1 / 720 + y * (1 / 40320))))
    odd = (turn & 1) == 1
    cos = jnp.where(odd, s, c)
    sin = jnp.where(odd, c, s)
    cos = jnp.where(((turn + 1) & 2) == 2, -cos, cos)
    sin = jnp.where((turn & 2) == 2, -sin, sin)
    return cos, sin


def kernel(first_ref, white_ref, coords_ref, slow_ref, out_ref, left, right, power):
    sources, bins, rows, width = white_ref.shape
    segs = rows // 2
    half = grid_size // 4
    norm = 1.0 / (sources * width * segs)
    sub = lax.broadcasted_iota(jnp.int32, (8, lane), 0)
    for f in range(bins):
        number = first_ref[0] + f
        for src in range(sources):
            for t in range(width // lane):
                at = pl.ds(src * width + t * lane, lane)
                east = jnp.broadcast_to(coords_ref[0:1, at], (8, lane)) * number
                north = jnp.broadcast_to(coords_ref[1:2, at], (8, lane)) * number
                ce, se = cos_sin(east)
                c8, _ = cos_sin(8 * north)
                step = 2 * c8
                tiles = [cos_sin(north * (sub + grid_low)), cos_sin(north * (sub + (grid_low + 8)))]
                for i in range(2, grid_size // 8):
                    tiles.append(tuple(step * a - b for a, b in zip(tiles[-1], tiles[-2])))
                for i in range(0, grid_size // 8, 2):
                    (c0, s0), (c1, s1) = tiles[i], tiles[i + 1]
                    here = pl.ds(8 * i, 16)
                    there = pl.ds(grid_size + 8 * i, 16)
                    right[f, here, at] = jnp.concatenate([c0, c1], 0).astype(jnp.bfloat16)
                    right[f, pl.ds(2 * grid_size + 8 * i, 16), at] = jnp.concatenate([s0, s1], 0).astype(jnp.bfloat16)
                    d0, d1 = c0 * ce - s0 * se, c1 * ce - s1 * se
                    r0, r1 = s0 * ce + c0 * se, s1 * ce + c1 * se
                    right[f, there, at] = jnp.concatenate([d0, d1], 0).astype(jnp.bfloat16)
                    right[f, pl.ds(3 * grid_size + 8 * i, 16), at] = jnp.concatenate([r0, r1], 0).astype(jnp.bfloat16)
                white = white_ref[src, f, :, pl.ds(t * lane, lane)]
                values = white.astype(jnp.float32)
                wr, wi = values[:segs], values[segs:]
                left[f, pl.ds(0, rows), at] = white
                ca, sa = 2 * ce * ce - 1, 2 * ce * se
                twice = 2 * ca
                cb, sb = jnp.ones_like(ca), jnp.zeros_like(sa)
                for a in range(1, half + 1):
                    base = rows * (2 * a - 1)
                    left[f, pl.ds(base, rows), at] = jnp.concatenate([wr * ca, wi * ca], 0).astype(jnp.bfloat16)
                    left[f, pl.ds(base + rows, rows), at] = jnp.concatenate([wr * sa, wi * sa], 0).astype(jnp.bfloat16)
                    ca, cb = twice * ca - cb, ca
                    sa, sb = twice * sa - sb, sa
        total = lax.dot_general(
            left[f], right[f], (((1,), (1,)), ((), ())), preferred_element_type=jnp.float32
        )

        def put(row, p, q):
            re = p[:, :lane] + q[:, lane:]
            im = q[:, :lane] - p[:, lane:]
            power[pl.ds(f * 2 * half + row, 1), :] = jnp.sum(re * re + im * im, axis=0, keepdims=True)

        put(half, total[:segs], total[segs:rows])
        for a in range(1, half + 1):
            base = rows * (2 * a - 1)
            cr, ci = total[base:base + segs], total[base + segs:base + rows]
            sr, si = total[base + rows:base + rows + segs], total[base + rows + segs:base + 2 * rows]
            put(half - a, cr - si, ci + sr)
            if a < half:
                put(half + a, cr + si, ci - sr)
    values = power[...] * norm
    high = values.astype(jnp.bfloat16)
    low = (values - high.astype(jnp.float32)).astype(jnp.bfloat16)
    pair = jnp.concatenate([high, low], 1)
    dests, _, beams = out_ref.shape
    for d in range(dests):
        at = pl.ds(d * beams, beams)
        east = slow_ref[0:1, at] - grid_low
        north = slow_ref[1:2, at] - grid_low
        column = (east & 1) * grid_size + north
        pick = lax.broadcasted_iota(jnp.int32, (lane, beams), 0) == column
        pick = jnp.where(pick, 1.0, 0.0).astype(jnp.bfloat16)
        found = jnp.dot(pair, jnp.concatenate([pick, pick], 0), preferred_element_type=jnp.float32)
        row = lax.broadcasted_iota(jnp.int32, (2 * half, beams), 0) == (east >> 1)
        for f in range(bins):
            part = jnp.where(row, found[f * 2 * half:(f + 1) * 2 * half], 0.0)
            out_ref[d, pl.ds(f, 1), :] = jnp.sum(part, axis=0, keepdims=True)


def beam_grid(first, white, coords, slowness, dests):
    sources, bins, rows, width = white.shape
    stations = sources * width
    beams = slowness.shape[1] // dests
    blocks = grid_size // 2 + 1
    vmem = pl.BlockSpec(memory_space=pltpu.VMEM)
    return pl.pallas_call(
        kernel,
        out_shape=jax.ShapeDtypeStruct((dests, bins, beams), jnp.float32),
        in_specs=[pl.BlockSpec(memory_space=pltpu.SMEM), vmem, vmem, vmem],
        out_specs=vmem,
        scratch_shapes=[
            pltpu.VMEM((bins, blocks * rows, stations), jnp.bfloat16),
            pltpu.VMEM((bins, 4 * grid_size, stations), jnp.bfloat16),
            pltpu.VMEM((bins * grid_size // 2, lane), jnp.float32),
        ],
        compiler_params=pltpu.CompilerParams(vmem_limit_bytes=48 * 1024 * 1024),
        name="beam_grid",
    )(first, white, coords, slowness)


def local(spectra, coords, slowness):
    bins_dev = spectra.shape[1]
    seg_count = spectra.shape[2]
    width = spectra.shape[3]
    peers = lax.axis_size("sta")
    groups = math.gcd(bins_dev, peers)
    copies = peers // groups
    bins_own = bins_dev // groups
    values = spectra.astype(jnp.float32)
    local_sq = jnp.sum(values * values, axis=(0, 1))
    total_bins = bins_dev * lax.axis_size("bins")
    totals = jnp.sum(lax.all_gather(local_sq, "bins"), axis=0)
    scale = jnp.sqrt(totals / (2 * total_bins) + epsilon)
    whitened = (values / scale).astype(jnp.bfloat16)
    parts = jnp.transpose(whitened.reshape(2, groups, bins_own, seg_count, width), (1, 2, 0, 3, 4))
    parts = parts.reshape(groups, bins_own, 2 * seg_count, width)
    if copies > 1:
        parts = jnp.repeat(parts, copies, axis=0)
    white = lax.all_to_all(parts, "sta", 0, 0, tiled=True)
    group = lax.axis_index("sta") // copies
    first = lax.axis_index("bins") * bins_dev + group * bins_own + 1
    powers = beam_grid(first.reshape(1).astype(jnp.int32), white, coords, slowness, peers)
    powers = lax.all_to_all(powers, "sta", 0, 0, tiled=True)
    return powers[::copies].reshape(bins_dev, -1)


def solution(mesh):
    in_specs = (P(None, "bins", None, "sta"), P(), P())
    out_specs = P("bins", "sta")
    return jax.shard_map(local, mesh=mesh, in_specs=in_specs, out_specs=out_specs, check_vma=False)
```

time: 471 us -> 42 us (0.09)
  other arithmetic: 334 us -> 1.17 us
  matrix products: 41.3 us -> 0 us
  waiting for transfers between devices: 49.2 us -> 9.41 us
  local copies, waits for them, and re-layouts: 23.8 us -> 1.35 us
  between operations: 13.5 us -> 0.04 us
  blocking collectives: 8.52 us -> 16.3 us
  Pallas kernels: 0 us -> 7.05 us
  starting transfers between devices: 0.01 us -> 6.42 us
    another operation x33 -> x0, other arithmetic: 328 us -> none
    all_gather x1 -> x0, waiting for transfers between devices: 49.1 us -> none  [local(): lax.all_gather(whitened, 'sta', axis=3, tiled=True)]
    dot_general x32 -> x0, matrix products: 41.3 us -> none  [one_bin(): lax.dot_general(steering, bin_rows, (((0,), (1,)), ((), ())), preferred_e...]
    dynamic_slice x32 -> x0, local copies, waits for them, and re-layouts: 19.9 us -> none  [one_block(): amps = lax.map(one_bin, (stacked, bin_numbers))]
    all_to_all x0 -> x1, blocking collectives: none -> 10.1 us  [local(): powers = lax.all_to_all(powers, 'sta', 0, 0, tiled=True)]
    all_to_all x0 -> x1, waiting for transfers between devices: none -> 9.41 us  [local(): white = lax.all_to_all(parts, 'sta', 0, 0, tiled=True)]
    psum x1 -> x0, blocking collectives: 8.52 us -> none  [local(): totals = lax.psum(local_sq, 'bins')]
    pallas_call x0 -> x1, Pallas kernels: none -> 7.05 us  [beam_grid(): pl.pallas_call(kernel, out_shape=jax.ShapeDtypeStruct((dests, bins, beams...]
where the time goes in v1:
time: 42 us; the launch traced here: 41.7 us
  blocking collectives  16.3 us (39%)
  waiting for transfers between devices  9.41 us (22%)
  Pallas kernels  7.05 us (17%)
  starting transfers between devices  6.42 us (15%)
  local copies, waits for them, and re-layouts  1.35 us (3%)
  other arithmetic  1.17 us (3%)
    all_to_all x1, blocking collectives, local(): powers = lax.all_to_all(powers, 'sta', 0, 0, tiled=True)  10.1 us
    all_to_all x1, waiting for transfers between devices, local(): white = lax.all_to_all(parts, 'sta', 0, 0, tiled=True)  9.41 us
    pallas_call x1, Pallas kernels, beam_grid(): pl.pallas_call(kernel, out_shape=jax.ShapeDtypeStruct((dests, bins, beams...  7.05 us
    all_to_all x1, starting transfers between devices, local(): white = lax.all_to_all(parts, 'sta', 0, 0, tiled=True)  6.42 us
    all_gather x1, blocking collectives, local(): totals = jnp.sum(lax.all_gather(local_sq, 'bins'), axis=0)  6.2 us
    reduce_sum x1, other arithmetic, local(): local_sq = jnp.sum(values * values, axis=(0, 1))  1.11 us
  transfers between devices with their start and end apart: 1, of which 1 were waited for; matrix products, arithmetic and copies ran while one was open for 0% of the time, Pallas kernels for 0%

profile of v1, /device:TPU:0, one launch (start us, length us, event | category | flops | bytes accessed | tf_op | source)
XLA Modules:
  0.0 41.7 jit_solution(2417787429171589721)
XLA Ops:
  0.0 0.0 copy-start.2
  0.0 1.1 %fusion = f32[8,256]{1,0:T(8,128)S(1)} fusion(bf16[2,32,8,256]{3,2,1,0:T(8,128)(2,1)} %param.3), kind=kLoop, calls=%fused_computation.2 | loop fusion | flops 391168 | bytes 270336 | tf_op jit(solution)/shard_map/reduce_sum | solution.py:144
  1.1 6.2 %all-gather = f32[32,256]{1,0:T(8,128)S(1)} all-gather(f32[8,256]{1,0:T(8,128)S(1)} %fusion), channel_id=2, replica_groups=mesh['bins'=4,'sta'=8] {'bins'}, dimensions={0}, use_global_device_ids=true | all-gather | bytes 40960 | tf_op jit(solution)/shard_map/all_gather | solution.py:146
  7.3 0.0 copy-done.2
  7.3 0.1 fusion.1
  7.4 0.7 %copy.7 = bf16[2,8,4,8,256]{4,3,0,2,1:T(8,128)(2,1)} copy(bf16[2,8,4,8,256]{4,3,2,1,0:T(8,128)(2,1)S(1)} %bitcast.9) | data formatting | bytes 524288 | tf_op jit(solution)/shard_map/reshape | solution.py:149
  8.1 0.0 copy-start.1
  8.1 6.4 %all-to-all-start = ((bf16[8,4,16,256]{3,2,1,0:T(8,128)(2,1)}), bf16[8,4,16,256]{3,2,1,0:T(8,128)(2,1)S(1)}, u32[]{:S(2)}, u32[]{:S(2)}) async-start(bf16[8,4,16,256]{3,2,1,0:T(8,128)(2,1)} %bitcast.8), calls=%async_computation | async-start | bytes 524288 | tf_op jit(solution)/shard_map/all_to_all | solution.py:153
  14.5 0.0 copy-start
  14.5 9.4 %all-to-all-done.white_ref = bf16[8,4,16,256]{3,2,1,0:T(8,128)(2,1)S(1)} async-done(((bf16[8,4,16,256]{3,2,1,0:T(8,128)(2,1)}), bf16[8,4,16,256]{3,2,1,0:T(8,128)(2,1)S(1)}, u32[]{:S(2)}, u32[]{:S(2)}) %all-to-all-start) | async-done | bytes 262176 | tf_op jit(solution)/shard_map/all_to_all | solution.py:153
  24.0 0.0 copy-done.1
  24.0 0.0 copy-done
  24.0 7.1 %beam_grid.1 = f32[8,4,256]{2,1,0:T(4,128)S(1)} custom-call(s32[1]{0:T(128)} %bitcast.first_ref, bf16[8,4,16,256]{3,2,1,0:T(8,128)(2,1)S(1)} %all-to-all-done.white_ref, s32[2,2048]{1,0:T(2,128)S(1)} %copy-done, s32[2,2048]{1,0:T(2,128)S(1)} %copy-done.1), custom_call_target="tpu_custom_call" | custom-call | tf_op jit(solution)/shard_map/beam_grid/pallas_call | solution.py:120
  31.0 10.1 %all_to_all.10 = f32[8,4,256]{2,1,0:T(4,128)S(1)} all-to-all(f32[8,4,256]{2,1,0:T(4,128)S(1)} %beam_grid.1), channel_id=1, replica_groups=mesh['bins'=4,'sta'=8] {'sta'}, dimensions={0} | all-to-all | bytes 65536 | tf_op jit(solution)/shard_map/all_to_all | solution.py:157
  41.1 0.6 %reshape.20 = f32[32,256]{1,0:T(8,128)} reshape(f32[8,4,256]{2,1,0:T(4,128)S(1)} %all_to_all.10) | data formatting | bytes 65536 | tf_op jit(solution)/shard_map/reshape | solution.py:158
  (2 shorter events, 0.0 us)
Async XLA Ops:
  0.0 7.3 %copy-start.2 = (bf16[2,32,8,256]{3,2,1,0:T(8,128)(2,1)S(1)}, bf16[2,32,8,256]{3,2,1,0:T(8,128)(2,1)}, u32[]{:S(2)}) copy-start(bf16[2,32,8,256]{3,2,1,0:T(8,128)(2,1)} %param.3) | copy-start | bytes 786436
  8.1 15.9 %copy-start.1 = (s32[2,2048]{1,0:T(2,128)S(1)}, s32[2,2048]{1,0:T(2,128)}, u32[]{:S(2)}) copy-start(s32[2,2048]{1,0:T(2,128)} %slow_ref.1) | copy-start | bytes 49156
  8.1 15.9 %all-to-all-start = ((bf16[8,4,16,256]{3,2,1,0:T(8,128)(2,1)}), bf16[8,4,16,256]{3,2,1,0:T(8,128)(2,1)S(1)}, u32[]{:S(2)}, u32[]{:S(2)}) async-start(bf16[8,4,16,256]{3,2,1,0:T(8,128)(2,1)} %bitcast.8), calls=%async_computation | async-start | bytes 524288 | tf_op jit(solution)/shard_map/all_to_all | solution.py:153
  14.5 9.4 %copy-start = (s32[2,2048]{1,0:T(2,128)S(1)}, s32[2,2048]{1,0:T(2,128)}, u32[]{:S(2)}) copy-start(s32[2,2048]{1,0:T(2,128)} %coords_ref.1) | copy-start | bytes 49156

commit v2 on v1

v2 whole, which is shorter than its diff:
```python
import functools
import math

import jax
import jax.numpy as jnp
from jax import lax
from jax.experimental import pallas as pl
from jax.experimental.pallas import tpu as pltpu
from jax.sharding import PartitionSpec as P

phase_modulus = 1048576
two_pi = 2.0 * math.pi
epsilon = 1e-06
grid_low = -32
grid_size = 64
lane = 128
vmem_limit = 32 * 1024 * 1024


def cos_sin(index):
    quarter = phase_modulus // 4
    shift = quarter.bit_length() - 1
    turn = (index + quarter // 2) >> shift
    rest = index - (turn << shift)
    x = rest.astype(jnp.float32) * (two_pi / phase_modulus)
    y = x * x
    s = x + x * y * (-1 / 6 + y * (1 / 120 + y * (-1 / 5040 + y * (1 / 362880))))
    c = 1 + y * (-1 / 2 + y * (1 / 24 + y * (-1 / 720 + y * (1 / 40320))))
    odd = (turn & 1) == 1
    cos = jnp.where(odd, s, c)
    sin = jnp.where(odd, c, s)
    cos = jnp.where(((turn + 1) & 2) == 2, -cos, cos)
    sin = jnp.where((turn & 2) == 2, -sin, sin)
    return cos, sin


def tables_kernel(first_ref, coords_ref, right_ref, factor_ref):
    stations = right_ref.shape[2]
    number = first_ref[0] + pl.program_id(0)
    sub = lax.broadcasted_iota(jnp.int32, (8, lane), 0)
    half = grid_size // 4

    def one(t):
        at = pl.ds(pl.multiple_of(t * lane, lane), lane)
        east = jnp.broadcast_to(coords_ref[0:1, at], (8, lane)) * number
        north = jnp.broadcast_to(coords_ref[1:2, at], (8, lane)) * number
        for i in range(0, half, 16):
            low, high = (cos_sin(east * (2 * (sub + j) + 1)) for j in (i, i + 8))
            factor_ref[0, pl.ds(i, 16), at] = jnp.concatenate([low[0], high[0]], 0).astype(jnp.bfloat16)
            factor_ref[0, pl.ds(half + i, 16), at] = jnp.concatenate([low[1], high[1]], 0).astype(jnp.bfloat16)
        ce, se = cos_sin(east)
        c8, _ = cos_sin(8 * north)
        step = 2 * c8
        tiles = [cos_sin(north * (sub + grid_low)), cos_sin(north * (sub + (grid_low + 8)))]
        for i in range(2, grid_size // 8):
            tiles.append(tuple(step * a - b for a, b in zip(tiles[-1], tiles[-2])))
        for i in range(0, grid_size // 8, 2):
            (c0, s0), (c1, s1) = tiles[i], tiles[i + 1]
            turned = [
                (c0 * ce + s0 * se, c1 * ce + s1 * se),
                (c0, c1),
                (s0 * ce - c0 * se, s1 * ce - c1 * se),
                (s0, s1),
            ]
            for block, halves in enumerate(turned):
                rows = pl.ds(block * grid_size + 8 * i, 16)
                right_ref[0, rows, at] = jnp.concatenate(halves, 0).astype(jnp.bfloat16)

    @pl.loop(0, stations // lane // 4)
    def _(t):
        for u in range(4):
            one(t * 4 + u)


def tables(first, coords, bins):
    stations = coords.shape[1]
    vmem = pl.BlockSpec(memory_space=pltpu.VMEM)
    return pl.pallas_call(
        tables_kernel,
        out_shape=(
            pltpu.HBM((bins, 4 * grid_size, stations), jnp.bfloat16),
            jax.ShapeDtypeStruct((bins, grid_size // 2, stations), jnp.bfloat16),
        ),
        grid=(bins,),
        in_specs=[pl.BlockSpec(memory_space=pltpu.SMEM), vmem],
        out_specs=(
            pl.BlockSpec((1, 4 * grid_size, stations), lambda f: (f, 0, 0)),
            pl.BlockSpec((1, grid_size // 2, stations), lambda f: (f, 0, 0)),
        ),
        compiler_params=pltpu.CompilerParams(vmem_limit_bytes=vmem_limit),
        cost_estimate=pl.CostEstimate(flops=bins * stations * 4096, bytes_accessed=bins * stations * 576, transcendentals=0),
        name="tables",
    )(first, coords)


def kernel(white_ref, right_hbm, factor_ref, slow_hbm, out_ref, left, right, wide, power, slow_ref, arrived, slow_in):
    sources, bins, rows, width = white_ref.shape
    segs = rows // 2
    half = grid_size // 4
    step = math.gcd(width, 2 * lane)
    norm = 1.0 / (sources * width * segs)
    copies = {}
    for f in range(0, bins, 2):
        for src in range(sources):
            at = (pl.ds(f, min(2, bins - f)), slice(None), pl.ds(src * width, width))
            copies[f, src] = pltpu.make_async_copy(right_hbm.at[at], right.at[at], arrived.at[f // 2, src])
            copies[f, src].start()
    slow_copy = pltpu.make_async_copy(slow_hbm, slow_ref, slow_in)
    slow_copy.start()
    def finish(f, total):
        def square(p, q):
            re = p[:, :2 * grid_size] + q[:, 2 * grid_size:]
            im = q[:, :2 * grid_size] - p[:, 2 * grid_size:]
            return re * re + im * im

        plus, minus = 0.0, 0.0
        for g in range(segs):
            rc, rs = (total[2 * half * g + half * i:][:half] for i in (0, 1))
            ic, im = (total[2 * half * (segs + g) + half * i:][:half] for i in (0, 1))
            plus += square(rc + im, ic - rs)
            minus += square(rc - im, ic + rs)
        power[pl.ds(f * 2 * half, half), :] = plus
        power[pl.ds(f * 2 * half + half, half), :] = minus

    def build(f, src):
        for t in range(width // step):
            at = pl.ds(src * width + t * step, step)
            wide[f, :, at] = white_ref[src, f, :, pl.ds(t * step, step)].astype(jnp.float32)
            cos, sin = factor_ref[f, :half, at], factor_ref[f, half:, at]
            for r in range(rows):
                value = jnp.broadcast_to(wide[f, r:r + 1, at], (half, step)).astype(jnp.bfloat16)
                left[f, pl.ds(2 * half * r, half), at] = cos * value
                left[f, pl.ds(2 * half * r + half, half), at] = sin * value

    for f in range(0, bins, 2):
        both = range(f, min(f + 2, bins))
        totals = [0.0] * len(both)
        for src in range(sources):
            for i in both:
                build(i, src)
            copies[f, src].wait()
            at = pl.ds(src * width, width)
            for i in both:
                totals[i - f] += lax.dot_general(
                    left[i, :, at], right[i, :, at], (((1,), (1,)), ((), ())), preferred_element_type=jnp.float32
                )
        for i in both:
            finish(i, totals[i - f])
    slow_copy.wait()
    values = power[...] * norm
    high = values.astype(jnp.bfloat16)
    low = (values - high.astype(jnp.float32)).astype(jnp.bfloat16)
    pair = jnp.concatenate([high, low], 1)
    dests, _, beams = out_ref.shape
    for d in range(dests):
        at = pl.ds(d * beams, beams)
        east = slow_ref[0:1, at]
        north = slow_ref[1:2, at] - grid_low
        column = (east & 1) * grid_size + north
        pick = lax.broadcasted_iota(jnp.int32, (2 * grid_size, beams), 0) == column
        pick = jnp.where(pick, 1.0, 0.0).astype(jnp.bfloat16)
        found = jnp.dot(pair, jnp.concatenate([pick, pick], 0), preferred_element_type=jnp.float32)
        east = jnp.where(east >= 0, east >> 1, half - 1 - (east >> 1))
        row = lax.broadcasted_iota(jnp.int32, (2 * half, beams), 0) == east
        for f in range(bins):
            part = jnp.where(row, found[f * 2 * half:(f + 1) * 2 * half], 0.0)
            out_ref[d, pl.ds(f, 1), :] = jnp.sum(part, axis=0, keepdims=True)


def beam_grid(white, right, factor, slowness, dests):
    sources, bins, rows, width = white.shape
    stations = sources * width
    beams = slowness.shape[1] // dests
    vmem = pl.BlockSpec(memory_space=pltpu.VMEM)
    hbm = pl.BlockSpec(memory_space=pltpu.HBM)
    pin = pltpu.with_memory_space_constraint
    return pl.pallas_call(
        kernel,
        out_shape=jax.ShapeDtypeStruct((dests, bins, beams), jnp.float32),
        in_specs=[vmem, hbm, vmem, hbm],
        out_specs=vmem,
        scratch_shapes=[
            pltpu.VMEM((bins, grid_size // 2 * rows, stations), jnp.bfloat16),
            pltpu.VMEM((bins, 4 * grid_size, stations), jnp.bfloat16),
            pltpu.VMEM((bins, rows, stations), jnp.float32),
            pltpu.VMEM((bins * grid_size // 2, 2 * grid_size), jnp.float32),
            pltpu.VMEM(slowness.shape, jnp.int32),
            pltpu.SemaphoreType.DMA((pl.cdiv(bins, 2), sources)),
            pltpu.SemaphoreType.DMA,
        ],
        compiler_params=pltpu.CompilerParams(vmem_limit_bytes=vmem_limit),
        cost_estimate=pl.CostEstimate(flops=bins * stations * 4096, bytes_accessed=bins * stations * 576, transcendentals=0),
        name="beam_grid",
    )(white, pin(right, pltpu.HBM), factor, pin(slowness, pltpu.HBM))


def local(spectra, coords, slowness):
    bins_dev = spectra.shape[1]
    seg_count = spectra.shape[2]
    width = spectra.shape[3]
    peers = lax.axis_size("sta")
    groups = math.gcd(bins_dev, peers)
    copies = peers // groups
    bins_own = bins_dev // groups
    values = spectra.astype(jnp.float32)
    local_sq = jnp.sum(values * values, axis=(0, 1))
    total_bins = bins_dev * lax.axis_size("bins")
    totals = jnp.sum(lax.all_gather(local_sq, "bins"), axis=0)
    scale = jnp.sqrt(totals / (2 * total_bins) + epsilon)
    whitened = (values / scale).astype(jnp.bfloat16)
    parts = jnp.transpose(whitened.reshape(2, groups, bins_own, seg_count, width), (1, 2, 0, 3, 4))
    parts = parts.reshape(groups, bins_own, 2 * seg_count, width)
    if copies > 1:
        parts = jnp.repeat(parts, copies, axis=0)
    white = lax.all_to_all(parts, "sta", 0, 0, tiled=True)
    group = lax.axis_index("sta") // copies
    first = lax.axis_index("bins") * bins_dev + group * bins_own + 1
    right, factor = tables(first.reshape(1).astype(jnp.int32), coords, bins_own)
    powers = beam_grid(white, right, factor, slowness, peers)
    powers = lax.all_to_all(powers, "sta", 0, 0, tiled=True)
    return powers[::copies].reshape(bins_dev, -1)


def solution(mesh):
    in_specs = (P(None, "bins", None, "sta"), P(), P())
    out_specs = P("bins", "sta")
    return jax.shard_map(local, mesh=mesh, in_specs=in_specs, out_specs=out_specs, check_vma=False)
```

time: 42 us -> 41.1 us (0.979)
  waiting for transfers between devices: 9.41 us -> 4.11 us
  Pallas kernels: 7.05 us -> 9.97 us
  other arithmetic: 1.17 us -> 2.05 us
  local copies, waits for them, and re-layouts: 1.35 us -> 2.05 us
    all_to_all x1, waiting for transfers between devices: 9.41 us -> 4.11 us  [local(): white = lax.all_to_all(parts, 'sta', 0, 0, tiled=True)]
    pallas_call x0 -> x1, Pallas kernels: none -> 4.6 us  [tables(): pl.pallas_call(tables_kernel, out_shape=(pltpu.HBM((bins, 4 * grid_size,...]
    pallas_call x1, Pallas kernels: 7.05 us -> 5.36 us  [beam_grid(): pl.pallas_call(kernel, out_shape=jax.ShapeDtypeStruct((dests, bins, beams...]
    convert_element_type x1, other arithmetic: 0.05 us -> 1 us  [local(): whitened = (values / scale).astype(jnp.bfloat16)]
    unnamed x6 -> x2, local copies, waits for them, and re-layouts: 0.01 us -> 0.71 us
  transfers between devices with their start and end apart: 1 -> 1, of which waited for: 1 -> 1; matrix products, arithmetic and copies ran while one was open for 0% -> 0% of each run, Pallas kernels for 0% -> 11%
where the time goes in v2:
time: 41.1 us; the launch traced here: 40.8 us
  blocking collectives  16.3 us (40%)
  Pallas kernels  9.97 us (24%)
  starting transfers between devices  6.29 us (15%)
  waiting for transfers between devices  4.11 us (10%)
  other arithmetic  2.05 us (5%)
  local copies, waits for them, and re-layouts  2.05 us (5%)
    all_to_all x1, blocking collectives, local(): powers = lax.all_to_all(powers, 'sta', 0, 0, tiled=True)  10.1 us
    all_to_all x1, starting transfers between devices, local(): white = lax.all_to_all(parts, 'sta', 0, 0, tiled=True)  6.29 us
    all_gather x1, blocking collectives, local(): totals = jnp.sum(lax.all_gather(local_sq, 'bins'), axis=0)  6.2 us
    pallas_call x1, Pallas kernels, beam_grid(): pl.pallas_call(kernel, out_shape=jax.ShapeDtypeStruct((dests, bins, beams...  5.36 us
    pallas_call x1, Pallas kernels, tables(): pl.pallas_call(tables_kernel, out_shape=(pltpu.HBM((bins, 4 * grid_size,...  4.6 us
    all_to_all x1, waiting for transfers between devices, local(): white = lax.all_to_all(parts, 'sta', 0, 0, tiled=True)  4.11 us
    reduce_sum x1, other arithmetic, local(): local_sq = jnp.sum(values * values, axis=(0, 1))  1.03 us
    convert_element_type x1, other arithmetic, local(): whitened = (values / scale).astype(jnp.bfloat16)  1 us
  transfers between devices with their start and end apart: 1, of which 1 were waited for; matrix products, arithmetic and copies ran while one was open for 0% of the time, Pallas kernels for 11%

profile of v2, /device:TPU:0, one launch (start us, length us, event | category | flops | bytes accessed | tf_op | source)
XLA Modules:
  0.0 40.8 jit_solution(6518702759142739530)
XLA Ops:
  0.0 1.0 %fusion = f32[8,256]{1,0:T(8,128)S(1)} fusion(bf16[2,32,8,256]{3,2,1,0:T(8,128)(2,1)} %param.3), kind=kLoop, calls=%fused_computation.2 | loop fusion | flops 391168 | bytes 270336 | tf_op jit(solution)/shard_map/reduce_sum | solution.py:206
  1.0 6.2 %all-gather = f32[32,256]{1,0:T(8,128)S(1)} all-gather(f32[8,256]{1,0:T(8,128)S(1)} %fusion), channel_id=2, replica_groups=mesh['bins'=4,'sta'=8] {'bins'}, dimensions={0}, use_global_device_ids=true | all-gather | bytes 40960 | tf_op jit(solution)/shard_map/all_gather | solution.py:208
  7.3 1.0 %fusion.1 = bf16[2,32,8,256]{3,2,1,0:T(8,128)(2,1)S(1)} fusion(bf16[2,32,8,256]{3,2,1,0:T(8,128)(2,1)} %param.3, f32[8,256]{1,0:T(8,128)S(1)} %add_sqrt_fusion), kind=kLoop, calls=%fused_computation.3 | loop fusion | flops 393216 | bytes 532480 | tf_op jit(solution)/shard_map/convert_element_type | solution.py:210
  8.3 0.7 %copy.7 = bf16[2,8,4,8,256]{4,3,0,2,1:T(8,128)(2,1)} copy(bf16[2,8,4,8,256]{4,3,2,1,0:T(8,128)(2,1)S(1)} %bitcast.9) | data formatting | bytes 524288 | tf_op jit(solution)/shard_map/reshape | solution.py:211
  9.0 6.3 %all-to-all-start = ((bf16[8,4,16,256]{3,2,1,0:T(8,128)(2,1)}), bf16[8,4,16,256]{3,2,1,0:T(8,128)(2,1)S(1)}, u32[]{:S(2)}, u32[]{:S(2)}) async-start(bf16[8,4,16,256]{3,2,1,0:T(8,128)(2,1)} %bitcast.8), calls=%async_computation | async-start | bytes 524288 | tf_op jit(solution)/shard_map/all_to_all | solution.py:215
  15.3 0.0 copy-start
  15.3 0.7 %copy-done = s32[2,2048]{1,0:T(2,128)S(1)} copy-done((s32[2,2048]{1,0:T(2,128)S(1)}, s32[2,2048]{1,0:T(2,128)}, u32[]{:S(2)}) %copy-start) | copy-done | bytes 16408
  16.0 4.6 %tables.1 = (bf16[4,256,2048]{2,1,0:T(8,128)(2,1)}, bf16[4,32,2048]{2,1,0:T(8,128)(2,1)S(1)}) custom-call(s32[1]{0:T(128)} %bitcast.4.first_ref, s32[2,2048]{1,0:T(2,128)S(1)} %copy-done), custom_call_target="tpu_custom_call" | custom-call | flops 33554432 | bytes 4718592 | tf_op jit(solution)/shard_map/tables/pallas_call | solution.py:78
  20.6 4.1 %all-to-all-done.white_ref = bf16[8,4,16,256]{3,2,1,0:T(8,128)(2,1)S(1)} async-done(((bf16[8,4,16,256]{3,2,1,0:T(8,128)(2,1)}), bf16[8,4,16,256]{3,2,1,0:T(8,128)(2,1)S(1)}, u32[]{:S(2)}, u32[]{:S(2)}) %all-to-all-start) | async-done | bytes 262176 | tf_op jit(solution)/shard_map/all_to_all | solution.py:215
  24.7 5.4 %beam_grid.1 = f32[8,4,256]{2,1,0:T(4,128)S(1)} custom-call(bf16[8,4,16,256]{3,2,1,0:T(8,128)(2,1)S(1)} %all-to-all-done.white_ref, bf16[4,256,2048]{2,1,0:T(8,128)(2,1)} %get-tuple-element.7.right_hbm, bf16[4,32,2048]{2,1,0:T(8,128)(2,1)S(1)} %get-tuple-element.8.factor_ref, s32[2,2048]{1,0:T(2,128)} %slow_hbm.1), custom_call_target="tpu_custom_call" | custom-call | flops 33554432 | bytes 4718592 | tf_op jit(solution)/shard_map/beam_grid/pallas_call | solution.py:177
  30.1 10.1 %all_to_all.10 = f32[8,4,256]{2,1,0:T(4,128)S(1)} all-to-all(f32[8,4,256]{2,1,0:T(4,128)S(1)} %beam_grid.1), channel_id=1, replica_groups=mesh['bins'=4,'sta'=8] {'sta'}, dimensions={0} | all-to-all | bytes 65536 | tf_op jit(solution)/shard_map/all_to_all | solution.py:220
  40.1 0.6 %reshape.20 = f32[32,256]{1,0:T(8,128)} reshape(f32[8,4,256]{2,1,0:T(4,128)S(1)} %all_to_all.10) | data formatting | bytes 65536 | tf_op jit(solution)/shard_map/reshape | solution.py:221
  (2 shorter events, 0.0 us)
Async XLA Ops:
  9.0 15.7 %all-to-all-start = ((bf16[8,4,16,256]{3,2,1,0:T(8,128)(2,1)}), bf16[8,4,16,256]{3,2,1,0:T(8,128)(2,1)S(1)}, u32[]{:S(2)}, u32[]{:S(2)}) async-start(bf16[8,4,16,256]{3,2,1,0:T(8,128)(2,1)} %bitcast.8), calls=%async_computation | async-start | bytes 524288 | tf_op jit(solution)/shard_map/all_to_all | solution.py:215
  15.3 0.7 %copy-start = (s32[2,2048]{1,0:T(2,128)S(1)}, s32[2,2048]{1,0:T(2,128)}, u32[]{:S(2)}) copy-start(s32[2,2048]{1,0:T(2,128)} %coords_ref.1) | copy-start | bytes 49156

commit v3 on v2

--- a/solution.py
+++ b/solution.py
@@ -78,7 +78,7 @@
     return pl.pallas_call(
         tables_kernel,
         out_shape=(
-            pltpu.HBM((bins, 4 * grid_size, stations), jnp.bfloat16),
+            jax.ShapeDtypeStruct((bins, 4 * grid_size, stations), jnp.bfloat16),
             jax.ShapeDtypeStruct((bins, grid_size // 2, stations), jnp.bfloat16),
         ),
         grid=(bins,),
@@ -93,18 +93,12 @@
     )(first, coords)
 
 
-def kernel(white_ref, right_hbm, factor_ref, slow_hbm, out_ref, left, right, wide, power, slow_ref, arrived, slow_in):
+def kernel(white_ref, right, factor_ref, slow_hbm, out_ref, left, wide, power, slow_ref, slow_in):
     sources, bins, rows, width = white_ref.shape
     segs = rows // 2
     half = grid_size // 4
     step = math.gcd(width, 2 * lane)
     norm = 1.0 / (sources * width * segs)
-    copies = {}
-    for f in range(0, bins, 2):
-        for src in range(sources):
-            at = (pl.ds(f, min(2, bins - f)), slice(None), pl.ds(src * width, width))
-            copies[f, src] = pltpu.make_async_copy(right_hbm.at[at], right.at[at], arrived.at[f // 2, src])
-            copies[f, src].start()
     slow_copy = pltpu.make_async_copy(slow_hbm, slow_ref, slow_in)
     slow_copy.start()
     def finish(f, total):
@@ -138,7 +132,6 @@
         for src in range(sources):
             for i in both:
                 build(i, src)
-            copies[f, src].wait()
             at = pl.ds(src * width, width)
             for i in both:
                 totals[i - f] += lax.dot_general(
@@ -177,21 +170,19 @@
     return pl.pallas_call(
         kernel,
         out_shape=jax.ShapeDtypeStruct((dests, bins, beams), jnp.float32),
-        in_specs=[vmem, hbm, vmem, hbm],
+        in_specs=[vmem, vmem, vmem, hbm],
         out_specs=vmem,
         scratch_shapes=[
             pltpu.VMEM((bins, grid_size // 2 * rows, stations), jnp.bfloat16),
-            pltpu.VMEM((bins, 4 * grid_size, stations), jnp.bfloat16),
             pltpu.VMEM((bins, rows, stations), jnp.float32),
             pltpu.VMEM((bins * grid_size // 2, 2 * grid_size), jnp.float32),
             pltpu.VMEM(slowness.shape, jnp.int32),
-            pltpu.SemaphoreType.DMA((pl.cdiv(bins, 2), sources)),
             pltpu.SemaphoreType.DMA,
         ],
         compiler_params=pltpu.CompilerParams(vmem_limit_bytes=vmem_limit),
         cost_estimate=pl.CostEstimate(flops=bins * stations * 4096, bytes_accessed=bins * stations * 576, transcendentals=0),
         name="beam_grid",
-    )(white, pin(right, pltpu.HBM), factor, pin(slowness, pltpu.HBM))
+    )(white, right, factor, pin(slowness, pltpu.HBM))
 
 
 def local(spectra, coords, slowness):
@@ -205,17 +196,21 @@
     values = spectra.astype(jnp.float32)
     local_sq = jnp.sum(values * values, axis=(0, 1))
     total_bins = bins_dev * lax.axis_size("bins")
-    totals = jnp.sum(lax.all_gather(local_sq, "bins"), axis=0)
+    rows = lax.axis_size("bins")
+    totals = local_sq
+    for shift in range(1, rows):
+        totals += lax.ppermute(local_sq, "bins", [(i, (i + shift) % rows) for i in range(rows)])
     scale = jnp.sqrt(totals / (2 * total_bins) + epsilon)
     whitened = (values / scale).astype(jnp.bfloat16)
     parts = jnp.transpose(whitened.reshape(2, groups, bins_own, seg_count, width), (1, 2, 0, 3, 4))
     parts = parts.reshape(groups, bins_own, 2 * seg_count, width)
     if copies > 1:
         parts = jnp.repeat(parts, copies, axis=0)
-    white = lax.all_to_all(parts, "sta", 0, 0, tiled=True)
     group = lax.axis_index("sta") // copies
     first = lax.axis_index("bins") * bins_dev + group * bins_own + 1
     right, factor = tables(first.reshape(1).astype(jnp.int32), coords, bins_own)
+    parts, right, factor = lax.optimization_barrier((parts, right, factor))
+    white = lax.all_to_all(parts, "sta", 0, 0, tiled=True)
     powers = beam_grid(white, right, factor, slowness, peers)
     powers = lax.all_to_all(powers, "sta", 0, 0, tiled=True)
     return powers[::copies].reshape(bins_dev, -1)

time: 41.1 us -> 39.9 us (0.971)
  blocking collectives: 16.3 us -> 26 us
  waiting for transfers between devices: 4.11 us -> 0.01 us
  Pallas kernels: 9.97 us -> 6.71 us
  starting transfers between devices: 6.29 us -> 3.24 us
  local copies, waits for them, and re-layouts: 2.05 us -> 1.36 us
    all_to_all x0 -> x1, blocking collectives: none -> 15.8 us  [local(): white = lax.all_to_all(parts, 'sta', 0, 0, tiled=True)]
    all_to_all x1 -> x0, starting transfers between devices: 6.29 us -> none  [local(): white = lax.all_to_all(parts, 'sta', 0, 0, tiled=True)]
    all_gather x1 -> x0, blocking collectives: 6.2 us -> none  [local(): totals = jnp.sum(lax.all_gather(local_sq, 'bins'), axis=0)]
    all_to_all x1 -> x0, waiting for transfers between devices: 4.11 us -> none  [local(): white = lax.all_to_all(parts, 'sta', 0, 0, tiled=True)]
    ppermute x0 -> x3, starting transfers between devices: none -> 3.24 us  [local(): lax.ppermute(local_sq, 'bins', [(i, (i + shift) % rows) for i in range(ro...]
    pallas_call x1, Pallas kernels: 5.36 us -> 3.25 us  [beam_grid(): pl.pallas_call(kernel, out_shape=jax.ShapeDtypeStruct((dests, bins, beams...]
    pallas_call x1, Pallas kernels: 4.6 us -> 3.46 us  [tables(): pl.pallas_call(tables_kernel, out_shape=(jax.ShapeDtypeStruct((bins, 4 *...]
    reshape x1, local copies, waits for them, and re-layouts: 0.71 us -> 0.02 us  [local(): whitened.reshape(2, groups, bins_own, seg_count, width)]
  transfers between devices with their start and end apart: 1 -> 3, of which waited for: 1 -> 0; matrix products, arithmetic and copies ran while one was open for 0% -> 0% of each run, Pallas kernels for 11% -> 9%
where the time goes in v3:
time: 39.9 us; the launch traced here: 39.5 us
  blocking collectives  26 us (65%)
  Pallas kernels  6.71 us (17%)
  starting transfers between devices  3.24 us (8%)
  other arithmetic  2.05 us (5%)
  local copies, waits for them, and re-layouts  1.36 us (3%)
    all_to_all x1, blocking collectives, local(): white = lax.all_to_all(parts, 'sta', 0, 0, tiled=True)  15.8 us
    all_to_all x1, blocking collectives, local(): powers = lax.all_to_all(powers, 'sta', 0, 0, tiled=True)  10.2 us
    pallas_call x1, Pallas kernels, tables(): pl.pallas_call(tables_kernel, out_shape=(jax.ShapeDtypeStruct((bins, 4 *...  3.46 us
    pallas_call x1, Pallas kernels, beam_grid(): pl.pallas_call(kernel, out_shape=jax.ShapeDtypeStruct((dests, bins, beams...  3.25 us
    ppermute x3, starting transfers between devices, local(): lax.ppermute(local_sq, 'bins', [(i, (i + shift) % rows) for i in range(ro...  3.24 us
    reduce_sum x1, other arithmetic, local(): local_sq = jnp.sum(values * values, axis=(0, 1))  1.03 us
    convert_element_type x1, other arithmetic, local(): whitened = (values / scale).astype(jnp.bfloat16)  1 us
  transfers between devices with their start and end apart: 3, of which 0 were waited for; matrix products, arithmetic and copies ran while one was open for 0% of the time, Pallas kernels for 9%

profile of v3, /device:TPU:0, one launch (start us, length us, event | category | flops | bytes accessed | tf_op | source)
XLA Modules:
  0.0 39.5 jit_solution(16192143753470858282)
XLA Ops:
  0.0 1.0 %fusion = f32[8,256]{1,0:T(8,128)S(1)} fusion(bf16[2,32,8,256]{3,2,1,0:T(8,128)(2,1)} %param.3), kind=kLoop, calls=%fused_computation.2 | loop fusion | flops 391168 | bytes 270336 | tf_op jit(solution)/shard_map/reduce_sum | solution.py:197
  1.0 2.5 %collective-permute-start.2 = (f32[8,256]{1,0:T(8,128)S(1)}, f32[8,256]{1,0:T(8,128)S(1)}, u32[]{:S(2)}, u32[]{:S(2)}) collective-permute-start(f32[8,256]{1,0:T(8,128)S(1)} %fusion), channel_id=1, source_target_pairs={{0,24},{8,0},{16,8},{24,16},{1,25},{9,1},{17,9},{25,17},{2,26},{10... | collective-permute-start | bytes 24584 | tf_op jit(solution)/shard_map/ppermute | solution.py:202
  3.5 0.6 %collective-permute-start.1 = (f32[8,256]{1,0:T(8,128)S(1)}, f32[8,256]{1,0:T(8,128)S(1)}, u32[]{:S(2)}, u32[]{:S(2)}) collective-permute-start(f32[8,256]{1,0:T(8,128)S(1)} %fusion), channel_id=1, source_target_pairs={{0,16},{8,24},{16,0},{24,8},{1,17},{9,25},{17,1},{25,9},{2,18},{10... | collective-permute-start | bytes 24584 | tf_op jit(solution)/shard_map/ppermute | solution.py:202
  4.1 0.2 collective-permute-start
  4.3 0.0 copy-start
  4.3 0.7 %copy-done = s32[2,2048]{1,0:T(2,128)S(1)} copy-done((s32[2,2048]{1,0:T(2,128)S(1)}, s32[2,2048]{1,0:T(2,128)}, u32[]{:S(2)}) %copy-start) | copy-done | bytes 16408
  5.0 3.5 %tables.1 = (bf16[4,256,2048]{2,1,0:T(8,128)(2,1)S(1)}, bf16[4,32,2048]{2,1,0:T(8,128)(2,1)S(1)}) custom-call(s32[1]{0:T(128)} %bitcast.3.first_ref, s32[2,2048]{1,0:T(2,128)S(1)} %copy-done), custom_call_target="tpu_custom_call" | custom-call | flops 33554432 | bytes 4718592 | tf_op jit(solution)/shard_map/tables/pallas_call | solution.py:78
  8.5 0.0 collective-permute-done.2
  8.5 0.0 collective-permute-done.1
  8.5 0.0 collective-permute-done
  8.5 1.0 %fusion.1 = bf16[2,32,8,256]{3,2,1,0:T(8,128)(2,1)S(1)} fusion(bf16[2,32,8,256]{3,2,1,0:T(8,128)(2,1)} %param.3, f32[8,256]{1,0:T(8,128)S(1)} %add_sqrt_fusion), kind=kLoop, calls=%fused_computation.3 | loop fusion | flops 393216 | bytes 532480 | tf_op jit(solution)/shard_map/convert_element_type | solution.py:204
  9.6 15.8 %all_to_all.10.white_ref = bf16[8,4,16,256]{3,2,1,0:T(8,128)(2,1)S(1)} all-to-all(bf16[8,4,16,256]{3,2,1,0:T(8,128)(2,1)S(1)} %bitcast.7), channel_id=1, replica_groups=mesh['bins'=4,'sta'=8] {'sta'}, dimensions={0} | all-to-all | bytes 524288 | tf_op jit(solution)/shard_map/all_to_all | solution.py:213
  25.4 3.3 %beam_grid.1 = f32[8,4,256]{2,1,0:T(4,128)S(1)} custom-call(bf16[8,4,16,256]{3,2,1,0:T(8,128)(2,1)S(1)} %all_to_all.10.white_ref, bf16[4,256,2048]{2,1,0:T(8,128)(2,1)S(1)} %get-tuple-element.13.right, bf16[4,32,2048]{2,1,0:T(8,128)(2,1)S(1)} %get-tuple-element.14.factor_ref, s32[2,2048]{1,0:T(2,128)} %slow_hbm.1), custom_call_target="tpu_custom_call" | custom-call | flops 33554432 | bytes 4718592 | tf_op jit(solution)/shard_map/beam_grid/pallas_call | solution.py:170
  28.6 10.2 %all_to_all.11 = f32[8,4,256]{2,1,0:T(4,128)S(1)} all-to-all(f32[8,4,256]{2,1,0:T(4,128)S(1)} %beam_grid.1), channel_id=1, replica_groups=mesh['bins'=4,'sta'=8] {'sta'}, dimensions={0} | all-to-all | bytes 65536 | tf_op jit(solution)/shard_map/all_to_all | solution.py:215
  38.8 0.6 %reshape.16 = f32[32,256]{1,0:T(8,128)} reshape(f32[8,4,256]{2,1,0:T(4,128)S(1)} %all_to_all.11) | data formatting | bytes 65536 | tf_op jit(solution)/shard_map/reshape | solution.py:216
  (2 shorter events, 0.0 us)
Async XLA Ops:
  1.0 7.4 %collective-permute-start.2 = (f32[8,256]{1,0:T(8,128)S(1)}, f32[8,256]{1,0:T(8,128)S(1)}, u32[]{:S(2)}, u32[]{:S(2)}) collective-permute-start(f32[8,256]{1,0:T(8,128)S(1)} %fusion), channel_id=1, source_target_pairs={{0,24},{8,0},{16,8},{24,16},{1,25},{9,1},{17,9},{25,17},{2,26},{10... | collective-permute-start | bytes 24584 | tf_op jit(solution)/shard_map/ppermute | solution.py:202
  3.5 5.0 %collective-permute-start.1 = (f32[8,256]{1,0:T(8,128)S(1)}, f32[8,256]{1,0:T(8,128)S(1)}, u32[]{:S(2)}, u32[]{:S(2)}) collective-permute-start(f32[8,256]{1,0:T(8,128)S(1)} %fusion), channel_id=1, source_target_pairs={{0,16},{8,24},{16,0},{24,8},{1,17},{9,25},{17,1},{25,9},{2,18},{10... | collective-permute-start | bytes 24584 | tf_op jit(solution)/shard_map/ppermute | solution.py:202
  4.1 4.4 %collective-permute-start = (f32[8,256]{1,0:T(8,128)S(1)}, f32[8,256]{1,0:T(8,128)S(1)}, u32[]{:S(2)}, u32[]{:S(2)}) collective-permute-start(f32[8,256]{1,0:T(8,128)S(1)} %fusion), channel_id=1, source_target_pairs={{0,8},{8,16},{16,24},{24,0},{1,9},{9,17},{17,25},{25,1},{2,10},{10... | collective-permute-start | bytes 24584 | tf_op jit(solution)/shard_map/ppermute | solution.py:202
  4.3 0.7 %copy-start = (s32[2,2048]{1,0:T(2,128)S(1)}, s32[2,2048]{1,0:T(2,128)}, u32[]{:S(2)}) copy-start(s32[2,2048]{1,0:T(2,128)} %coords_ref.1) | copy-start | bytes 49156

commit v4 on v3

v4 whole, which is shorter than its diff:
```python
import math

import jax
import jax.numpy as jnp
from jax import lax
from jax.experimental import pallas as pl
from jax.experimental.pallas import tpu as pltpu
from jax.sharding import PartitionSpec as P


phase_modulus = 1048576
epsilon = 1e-06
grid_half = 32
lefts = grid_half // 4
lane = 128
vmem_limit = 32 * 1024 * 1024


def cos_sin(index):
    quarter = phase_modulus // 2
    shift = quarter.bit_length() - 1
    turn = (index + quarter // 2) >> shift
    rest = index - (turn << shift)
    x = rest.astype(jnp.float32) * (math.pi / phase_modulus)
    y = x * x
    s = x + x * y * (-1.6666654611e-1 + y * (8.3321608736e-3 + y * -1.9515295891e-4))
    c = 1 - 0.5 * y + y * y * (4.166664568298827e-2 + y * (-1.388731625493765e-3 + y * 2.443315711809948e-5))
    odd = (turn & 1) == 1
    cos = jnp.where(odd, s, c)
    sin = jnp.where(odd, c, s)
    cos = jnp.where(((turn + 1) & 2) == 2, -cos, cos)
    sin = jnp.where((turn & 2) == 2, -sin, sin)
    return cos, sin


def sums_kernel(spectra_hbm, coords_hbm, slow_hbm, sums_ref, spectra_ref, coords_ref, slow_ref, arrived, small):
    bins = spectra_ref.shape[1]
    piece = math.gcd(bins, 8)
    copies = []
    for i in range(bins // piece):
        at = (slice(None), pl.ds(i * piece, piece))
        copies.append(pltpu.make_async_copy(spectra_hbm.at[at], spectra_ref.at[at], arrived.at[i]))
    copies.append(pltpu.make_async_copy(coords_hbm, coords_ref, small.at[0]))
    copies.append(pltpu.make_async_copy(slow_hbm, slow_ref, small.at[1]))
    for copy in copies:
        copy.start()
    total = 0.0
    for i in range(bins // piece):
        copies[i].wait()
        for f in range(i * piece, (i + 1) * piece):
            for c in range(2):
                values = spectra_ref[c, f].astype(jnp.float32)
                total += values * values
    sums_ref[...] = total
    for copy in copies[bins // piece:]:
        copy.wait()


def sums(spectra, coords, slowness):
    hbm = pl.BlockSpec(memory_space=pltpu.HBM)
    vmem = pl.BlockSpec(memory_space=pltpu.VMEM)
    return pl.pallas_call(
        sums_kernel,
        out_shape=(
            jax.ShapeDtypeStruct(spectra.shape[2:], jnp.float32),
            jax.ShapeDtypeStruct(spectra.shape, spectra.dtype),
            jax.ShapeDtypeStruct(coords.shape, coords.dtype),
            jax.ShapeDtypeStruct(slowness.shape, slowness.dtype),
        ),
        in_specs=[hbm] * 3,
        out_specs=(vmem,) * 4,
        scratch_shapes=[
            pltpu.SemaphoreType.DMA((spectra.shape[1] // math.gcd(spectra.shape[1], 8),)),
            pltpu.SemaphoreType.DMA((2,)),
        ],
        compiler_params=pltpu.CompilerParams(vmem_limit_bytes=vmem_limit),
        cost_estimate=pl.CostEstimate(flops=2 * spectra.size, bytes_accessed=2 * spectra.size, transcendentals=0),
        name="sums",
    )(*(pltpu.with_memory_space_constraint(a, pltpu.HBM) for a in (spectra, coords, slowness)))


def tables_kernel(groups, coords_ref, right_ref, factor_ref, turn_ref):
    bins, columns, stations = right_ref.shape
    _, bins_dev, width = turn_ref.shape
    own = lax.axis_index("sta")
    row_first = lax.axis_index("bins") * bins_dev + 1
    first = row_first + own // (lax.axis_size("sta") // groups) * bins
    mine = pl.ds(pl.multiple_of(own * width, lane), width)
    both = coords_ref[0:1, mine] + coords_ref[1:2, mine]
    piece = math.gcd(bins_dev, 8)
    for i in range(0, bins_dev, piece):
        number = row_first + i + lax.broadcasted_iota(jnp.int32, (piece, width), 0)
        cos, sin = cos_sin(number * both)
        turn_ref[0, pl.ds(i, piece), :] = cos
        turn_ref[1, pl.ds(i, piece), :] = sin

    step = math.gcd(stations, 2 * lane)
    blocks = stations // step
    sub = lax.broadcasted_iota(jnp.int32, (8, step), 0)

    @pl.loop(0, bins * blocks)
    def _(item):
        f = item // blocks
        at = pl.ds(pl.multiple_of(lax.rem(item, blocks) * step, step), step)
        number = first + f
        east = jnp.broadcast_to(coords_ref[0:1, at], (8, step)) * number
        north = jnp.broadcast_to(coords_ref[1:2, at], (8, step)) * number
        factor_ref[f, :, at] = jnp.concatenate(cos_sin(east * (8 * sub + 4)), 0).astype(jnp.bfloat16)
        twice = 2 * cos_sin(16 * north)[0]
        c2, s2 = cos_sin(2 * east)
        start = [cos_sin(east + north * (2 * sub + odd)) for odd in (1 - 2 * grid_half, 17 - 2 * grid_half)]
        turned = [(c * c2 - s * s2, s * c2 + c * s2) for c, s in start]
        for d, (one, two) in enumerate((start, turned)):
            for i in range(0, 2 * grid_half, 16):
                for part in range(2):
                    rows = pl.ds((2 * part + d) * 2 * grid_half + i, 16)
                    right_ref[f, rows, at] = jnp.concatenate([one[part], two[part]], 0).astype(jnp.bfloat16)
                one = tuple(twice * b - a for a, b in zip(one, two))
                two = tuple(twice * b - a for a, b in zip(two, one))


def tables(coords, bins, groups, bins_dev, width):
    stations = coords.shape[1]
    vmem = pl.BlockSpec(memory_space=pltpu.VMEM)
    return pl.pallas_call(
        lambda *refs: tables_kernel(groups, *refs),
        out_shape=(
            jax.ShapeDtypeStruct((bins, 8 * grid_half, stations), jnp.bfloat16),
            jax.ShapeDtypeStruct((bins, 2 * lefts, stations), jnp.bfloat16),
            jax.ShapeDtypeStruct((2, bins_dev, width), jnp.float32),
        ),
        in_specs=[vmem],
        out_specs=(vmem,) * 3,
        compiler_params=pltpu.CompilerParams(vmem_limit_bytes=vmem_limit),
        cost_estimate=pl.CostEstimate(flops=bins * stations * 4096, bytes_accessed=bins * stations * 576, transcendentals=0),
        name="tables",
    )(coords)


def whiten_kernel(total_bins, spectra_ref, turn_ref, *refs):
    *sums_refs, out_ref = refs
    groups, bins, rows, width = out_ref.shape
    total = sum(ref[...] for ref in sums_refs)
    inverse = 1.0 / jnp.sqrt(total / (2 * total_bins) + epsilon)
    for i in range(groups * bins):
        wr = spectra_ref[0, i].astype(jnp.float32) * inverse
        wi = spectra_ref[1, i].astype(jnp.float32) * inverse
        cos, sin = turn_ref[0, i:i + 1, :], turn_ref[1, i:i + 1, :]
        both = jnp.concatenate([wr * cos - wi * sin, wi * cos + wr * sin], 0)
        out_ref[i // bins, i % bins] = both.astype(jnp.bfloat16)


def whiten(spectra, turn, partial, total_bins, groups):
    _, bins_dev, segs, width = spectra.shape
    vmem = pl.BlockSpec(memory_space=pltpu.VMEM)
    return pl.pallas_call(
        lambda *refs: whiten_kernel(total_bins, *refs),
        out_shape=jax.ShapeDtypeStruct((groups, bins_dev // groups, 2 * segs, width), jnp.bfloat16),
        in_specs=[vmem] * (2 + len(partial)),
        out_specs=vmem,
        compiler_params=pltpu.CompilerParams(vmem_limit_bytes=vmem_limit),
        cost_estimate=pl.CostEstimate(flops=8 * spectra.size, bytes_accessed=4 * spectra.size, transcendentals=0),
        name="whiten",
    )(spectra, turn, *partial)


def grid_kernel(white_ref, right_ref, factor_ref, slow_ref, out_ref, left, power):
    sources, bins, rows, width = white_ref.shape
    segs = rows // 2
    basis = 2 * lefts
    step = math.gcd(width, 2 * lane)
    norm = 1.0 / (sources * width * segs)
    columns = 4 * grid_half

    def build(f, src):
        for t in range(width // step):
            at = pl.ds(src * width + t * step, step)
            white = white_ref[src, f, :, pl.ds(t * step, step)].astype(jnp.float32)
            factor = factor_ref[f, :, at]
            for r in range(rows):
                value = jnp.broadcast_to(white[r:r + 1], (basis, step)).astype(jnp.bfloat16)
                left[f, pl.ds(basis * r, basis), at] = factor * value

    def finish(f, total):
        found = [0.0] * 4
        for g in range(segs):
            real = total[basis * g:basis * (g + 1)]
            imag = total[basis * (segs + g):basis * (segs + g + 1)]
            rcc, rcs = real[:lefts, :columns], real[:lefts, columns:]
            rsc, rss = real[lefts:, :columns], real[lefts:, columns:]
            icc, ics = imag[:lefts, :columns], imag[:lefts, columns:]
            isc, iss = imag[lefts:, :columns], imag[lefts:, columns:]
            same = (rcc - rss, isc + ics, icc - iss, rsc + rcs)
            mixed = (rcc + rss, isc - ics, icc + iss, rsc - rcs)
            for q, (a, b, c, d) in ((0, same), (2, mixed)):
                found[q] += (a + b) * (a + b) + (c - d) * (c - d)
                found[q + 1] += (a - b) * (a - b) + (c + d) * (c + d)
        for q in range(4):
            power[pl.ds((4 * f + q) * lefts, lefts), :] = found[q] * norm

    for f in range(0, bins, 2):
        both = range(f, min(f + 2, bins))
        totals = [0.0] * len(both)
        for src in range(sources):
            for i in both:
                build(i, src)
            at = pl.ds(src * width, width)
            for i in both:
                totals[i - f] += lax.dot_general(
                    left[i, :, at], right_ref[i, :, at], (((1,), (1,)), ((), ())), preferred_element_type=jnp.float32
                )
        for i in both:
            finish(i, totals[i - f])

    values = power[...]
    high = values.astype(jnp.bfloat16)
    low = (values - high.astype(jnp.float32)).astype(jnp.bfloat16)
    pair = jnp.concatenate([high, low], 1)
    dests, _, beams = out_ref.shape
    for d in range(dests):
        at = pl.ds(d * beams, beams)
        east = 2 * slow_ref[0:1, at] + 1
        north = slow_ref[1:2, at]
        size = jnp.abs(east)
        place = (size & 7) >> 1
        positive = east > 0
        same = positive == (place >= 2)
        column = jnp.where(same, north + grid_half, grid_half - 1 - north)
        column += jnp.where((place == 1) | (place == 2), 0, 2 * grid_half)
        sign = jnp.where(place >= 2, jnp.where(positive, 0, 1), jnp.where(positive, 2, 3))
        wanted = sign * lefts + (size >> 3)
        pick = lax.broadcasted_iota(jnp.int32, (columns, beams), 0) == column
        pick = jnp.where(pick, 1.0, 0.0).astype(jnp.bfloat16)
        found = jnp.dot(pair, jnp.concatenate([pick, pick], 0), preferred_element_type=jnp.float32)
        row = lax.broadcasted_iota(jnp.int32, (4 * lefts, beams), 0) == wanted
        for f in range(bins):
            part = jnp.where(row, found[f * 4 * lefts:(f + 1) * 4 * lefts], 0.0)
            out_ref[d, pl.ds(f, 1), :] = jnp.sum(part, axis=0, keepdims=True)


def beam_grid(white, right, factor, slowness, dests):
    sources, bins, rows, width = white.shape
    stations = sources * width
    beams = slowness.shape[1] // dests
    vmem = pl.BlockSpec(memory_space=pltpu.VMEM)
    return pl.pallas_call(
        grid_kernel,
        out_shape=jax.ShapeDtypeStruct((dests, bins, beams), jnp.float32),
        in_specs=[vmem] * 4,
        out_specs=vmem,
        scratch_shapes=[
            pltpu.VMEM((bins, 2 * lefts * rows, stations), jnp.bfloat16),
            pltpu.VMEM((bins * 4 * lefts, 4 * grid_half), jnp.float32),
        ],
        compiler_params=pltpu.CompilerParams(vmem_limit_bytes=vmem_limit),
        cost_estimate=pl.CostEstimate(flops=bins * stations * 4096, bytes_accessed=bins * stations * 576, transcendentals=0),
        name="beam_grid",
    )(white, right, factor, slowness)


def local(spectra, coords, slowness):
    _, bins_dev, _, width = spectra.shape
    peers = lax.axis_size("sta")
    rows = lax.axis_size("bins")
    groups = math.gcd(bins_dev, peers)
    copies = peers // groups
    bins_own = bins_dev // groups
    local_sq, spectra, coords, slowness = sums(spectra, coords, slowness)
    partial = [local_sq]
    for shift in range(1, rows):
        partial.append(lax.ppermute(local_sq, "bins", [(i, (i + shift) % rows) for i in range(rows)]))
    right, factor, turn = tables(coords, bins_own, groups, bins_dev, width)
    parts = whiten(spectra, turn, partial, bins_dev * rows, groups)
    if copies > 1:
        parts = jnp.repeat(parts, copies, axis=0)
    white = lax.all_to_all(parts, "sta", 0, 0, tiled=True)
    powers = beam_grid(white, right, factor, slowness, peers)
    powers = lax.all_to_all(powers, "sta", 0, 0, tiled=True)
    return powers[::copies].reshape(bins_dev, -1)


def solution(mesh):
    in_specs = (P(None, "bins", None, "sta"), P(), P())
    out_specs = P("bins", "sta")
    return jax.shard_map(local, mesh=mesh, in_specs=in_specs, out_specs=out_specs, check_vma=False)
```

time: 39.9 us -> 36 us (0.902)
  other arithmetic: 2.05 us -> 0 us
  Pallas kernels: 6.71 us -> 5.64 us
  local copies, waits for them, and re-layouts: 1.36 us -> 0.63 us
    pallas_call x2 -> x4, Pallas kernels: 6.71 us -> 5.64 us  [the longest x1 2.79 us: tables(): pl.pallas_call(lambda *refs: tables_kernel(groups, *refs), out_shape=(jax...]
    reduce_sum x1 -> x0, other arithmetic: 1.03 us -> none  [local(): local_sq = jnp.sum(values * values, axis=(0, 1))]
    convert_element_type x1 -> x0, other arithmetic: 1 us -> none  [local(): whitened = (values / scale).astype(jnp.bfloat16)]
    unnamed x2 -> x0, local copies, waits for them, and re-layouts: 0.72 us -> none
  transfers between devices with their start and end apart: 3 -> 3, of which waited for: 0 -> 2; matrix products, arithmetic and copies ran while one was open for 0% -> 0% of each run, Pallas kernels for 9% -> 8%
where the time goes in v4:
time: 36 us; the launch traced here: 35.8 us
  blocking collectives  26.1 us (72%)
  Pallas kernels  5.64 us (16%)
  starting transfers between devices  3.25 us (9%)
  local copies, waits for them, and re-layouts  0.63 us (2%)
    all_to_all x1, blocking collectives, local(): white = lax.all_to_all(parts, 'sta', 0, 0, tiled=True)  15.9 us
    all_to_all x1, blocking collectives, local(): powers = lax.all_to_all(powers, 'sta', 0, 0, tiled=True)  10.2 us
    ppermute x3, starting transfers between devices, local(): lax.ppermute(local_sq, 'bins', [(i, (i + shift) % rows) for i in range(ro...  3.25 us
    pallas_call x1, Pallas kernels, tables(): pl.pallas_call(lambda *refs: tables_kernel(groups, *refs), out_shape=(jax...  2.79 us
    pallas_call x1, Pallas kernels, beam_grid(): pl.pallas_call(grid_kernel, out_shape=jax.ShapeDtypeStruct((dests, bins,...  1.72 us
    pallas_call x1, Pallas kernels, sums(): pl.pallas_call(sums_kernel, out_shape=(jax.ShapeDtypeStruct(spectra.shape...  1.02 us
  transfers between devices with their start and end apart: 3, of which 2 were waited for; matrix products, arithmetic and copies ran while one was open for 0% of the time, Pallas kernels for 8%

profile of v4, /device:TPU:0, one launch (start us, length us, event | category | flops | bytes accessed | tf_op | source)
XLA Modules:
  0.0 35.8 jit_solution(2604525838000928831)
XLA Ops:
  0.0 1.0 %sums.1 = (f32[8,256]{1,0:T(8,128)S(1)}, bf16[2,32,8,256]{3,2,1,0:T(8,128)(2,1)S(1)}, s32[2,2048]{1,0:T(2,128)S(1)}, s32[2,2048]{1,0:T(2,128)S(1)}) custom-call(bf16[2,32,8,256]{3,2,1,0:T(8,128)(2,1)} %spectra_hbm.1, s32[2,2048]{1,0:T(2,128)} %coords_hbm.1, s32[2,2048]{1,0:T(2,128)} %slow_hbm.1), custom_call_target="tpu_custom_call" | custom-call | flops 262144 | bytes 262144 | tf_op jit(solution)/shard_map/sums/pallas_call | solution.py:62
  1.0 2.5 %collective-permute-start.2 = (f32[8,256]{1,0:T(8,128)S(1)}, f32[8,256]{1,0:T(8,128)S(1)}, u32[]{:S(2)}, u32[]{:S(2)}) collective-permute-start(f32[8,256]{1,0:T(8,128)S(1)} %get-tuple-element.15.refs_2_), channel_id=1, source_target_pairs={{0,24},{8,0},{16,8},{24,16},{1,25},{9,1},{17,9},{25,17},{2,26},{10... | collective-permute-start | bytes 24584 | tf_op jit(solution)/shard_map/ppermute | solution.py:271
  3.5 0.6 %collective-permute-start.1 = (f32[8,256]{1,0:T(8,128)S(1)}, f32[8,256]{1,0:T(8,128)S(1)}, u32[]{:S(2)}, u32[]{:S(2)}) collective-permute-start(f32[8,256]{1,0:T(8,128)S(1)} %get-tuple-element.15.refs_2_), channel_id=1, source_target_pairs={{0,16},{8,24},{16,0},{24,8},{1,17},{9,25},{17,1},{25,9},{2,18},{10... | collective-permute-start | bytes 24584 | tf_op jit(solution)/shard_map/ppermute | solution.py:271
  4.1 0.2 collective-permute-start
  4.3 2.8 %tables.1 = (bf16[4,256,2048]{2,1,0:T(8,128)(2,1)S(1)}, bf16[4,16,2048]{2,1,0:T(8,128)(2,1)S(1)}, f32[2,32,256]{2,1,0:T(8,128)S(1)}) custom-call(s32[2,2048]{1,0:T(2,128)S(1)} %get-tuple-element.13.refs_0_), custom_call_target="tpu_custom_call" | custom-call | flops 33554432 | bytes 4718592 | tf_op jit(solution)/shard_map/tables/pallas_call | solution.py:125
  7.1 0.0 collective-permute-done.2.refs_5_
  7.1 0.1 collective-permute-done.1.refs_4_
  7.2 0.1 collective-permute-done.refs_3_
  7.2 0.1 whiten.1
  7.3 15.9 %all_to_all.10.white_ref = bf16[8,4,16,256]{3,2,1,0:T(8,128)(2,1)S(1)} all-to-all(bf16[8,4,16,256]{3,2,1,0:T(8,128)(2,1)S(1)} %whiten.1), channel_id=1, replica_groups=mesh['bins'=4,'sta'=8] {'sta'}, dimensions={0} | all-to-all | bytes 524288 | tf_op jit(solution)/shard_map/all_to_all | solution.py:276
  23.2 1.7 %beam_grid.1 = f32[8,4,256]{2,1,0:T(4,128)S(1)} custom-call(bf16[8,4,16,256]{3,2,1,0:T(8,128)(2,1)S(1)} %all_to_all.10.white_ref, bf16[4,256,2048]{2,1,0:T(8,128)(2,1)S(1)} %get-tuple-element.16.right_ref, bf16[4,16,2048]{2,1,0:T(8,128)(2,1)S(1)} %get-tuple-element.17.factor_ref, s32[2,2048]{1,0:T(2,128)S(1)} %get-tuple-element.18.slow_ref), custom_call_target="tpu_custom_call" | custom-call | flops 33554432 | bytes 4718592 | tf_op jit(solution)/shard_map/beam_grid/pallas_call | solution.py:246
  25.0 10.2 %all_to_all.11 = f32[8,4,256]{2,1,0:T(4,128)S(1)} all-to-all(f32[8,4,256]{2,1,0:T(4,128)S(1)} %beam_grid.1), channel_id=1, replica_groups=mesh['bins'=4,'sta'=8] {'sta'}, dimensions={0} | all-to-all | bytes 65536 | tf_op jit(solution)/shard_map/all_to_all | solution.py:278
  35.1 0.6 %reshape.3 = f32[32,256]{1,0:T(8,128)} reshape(f32[8,4,256]{2,1,0:T(4,128)S(1)} %all_to_all.11) | data formatting | bytes 65536 | tf_op jit(solution)/shard_map/reshape | solution.py:279
Async XLA Ops:
  1.0 6.0 %collective-permute-start.2 = (f32[8,256]{1,0:T(8,128)S(1)}, f32[8,256]{1,0:T(8,128)S(1)}, u32[]{:S(2)}, u32[]{:S(2)}) collective-permute-start(f32[8,256]{1,0:T(8,128)S(1)} %get-tuple-element.15.refs_2_), channel_id=1, source_target_pairs={{0,24},{8,0},{16,8},{24,16},{1,25},{9,1},{17,9},{25,17},{2,26},{10... | collective-permute-start | bytes 24584 | tf_op jit(solution)/shard_map/ppermute | solution.py:271
  3.5 3.7 %collective-permute-start.1 = (f32[8,256]{1,0:T(8,128)S(1)}, f32[8,256]{1,0:T(8,128)S(1)}, u32[]{:S(2)}, u32[]{:S(2)}) collective-permute-start(f32[8,256]{1,0:T(8,128)S(1)} %get-tuple-element.15.refs_2_), channel_id=1, source_target_pairs={{0,16},{8,24},{16,0},{24,8},{1,17},{9,25},{17,1},{25,9},{2,18},{10... | collective-permute-start | bytes 24584 | tf_op jit(solution)/shard_map/ppermute | solution.py:271
  4.1 3.1 %collective-permute-start = (f32[8,256]{1,0:T(8,128)S(1)}, f32[8,256]{1,0:T(8,128)S(1)}, u32[]{:S(2)}, u32[]{:S(2)}) collective-permute-start(f32[8,256]{1,0:T(8,128)S(1)} %get-tuple-element.15.refs_2_), channel_id=1, source_target_pairs={{0,8},{8,16},{16,24},{24,0},{1,9},{9,17},{17,25},{25,1},{2,10},{10... | collective-permute-start | bytes 24584 | tf_op jit(solution)/shard_map/ppermute | solution.py:271

commit v5 on v4

--- a/solution.py
+++ b/solution.py
@@ -17,20 +17,20 @@
 
 
 def cos_sin(index):
-    quarter = phase_modulus // 2
-    shift = quarter.bit_length() - 1
-    turn = (index + quarter // 2) >> shift
-    rest = index - (turn << shift)
-    x = rest.astype(jnp.float32) * (math.pi / phase_modulus)
+    shift = 33 - (2 * phase_modulus).bit_length()
+    rest = (index << shift) >> shift
+    x = rest.astype(jnp.float32) * (math.pi / (4 * phase_modulus))
     y = x * x
-    s = x + x * y * (-1.6666654611e-1 + y * (8.3321608736e-3 + y * -1.9515295891e-4))
-    c = 1 - 0.5 * y + y * y * (4.166664568298827e-2 + y * (-1.388731625493765e-3 + y * 2.443315711809948e-5))
-    odd = (turn & 1) == 1
-    cos = jnp.where(odd, s, c)
-    sin = jnp.where(odd, c, s)
-    cos = jnp.where(((turn + 1) & 2) == 2, -cos, cos)
-    sin = jnp.where((turn & 2) == 2, -sin, sin)
+    sin = x + x * y * (-1.6666654611e-1 + y * (8.3321608736e-3 + y * -1.9515295891e-4))
+    cos = 1 - 0.5 * y + y * y * (4.166664568298827e-2 + y * (-1.388731625493765e-3 + y * 2.443315711809948e-5))
+    for _ in range(2):
+        twice = sin + sin
+        cos, sin = 1 - twice * sin, twice * cos
     return cos, sin
+
+
+def rotate(one, two):
+    return one[0] * two[0] - one[1] * two[1], one[1] * two[0] + one[0] * two[1]
 
 
 def sums_kernel(spectra_hbm, coords_hbm, slow_hbm, sums_ref, spectra_ref, coords_ref, slow_ref, arrived, small):
@@ -79,7 +79,7 @@
     )(*(pltpu.with_memory_space_constraint(a, pltpu.HBM) for a in (spectra, coords, slowness)))
 
 
-def tables_kernel(groups, coords_ref, right_ref, factor_ref, turn_ref):
+def tables_kernel(groups, coords_ref, slow_ref, right_ref, factor_ref, turn_ref, pick_ref, wanted_ref, rows_ref):
     bins, columns, stations = right_ref.shape
     _, bins_dev, width = turn_ref.shape
     own = lax.axis_index("sta")
@@ -94,47 +94,80 @@
         turn_ref[0, pl.ds(i, piece), :] = cos
         turn_ref[1, pl.ds(i, piece), :] = sin
 
+    beams = slow_ref.shape[1]
+    columns = 4 * grid_half
+    piece = math.gcd(beams, 2 * lane)
+    for i in range(0, beams, piece):
+        at = pl.ds(i, piece)
+        east = 2 * slow_ref[0:1, at] + 1
+        north = slow_ref[1:2, at]
+        size = jnp.abs(east)
+        place = (size & 7) >> 1
+        positive = east > 0
+        same = positive == (place >= 2)
+        column = jnp.where(same, north + grid_half, grid_half - 1 - north)
+        column += jnp.where((place == 1) | (place == 2), 0, 2 * grid_half)
+        sign = jnp.where(place >= 2, jnp.where(positive, 0, 1), jnp.where(positive, 2, 3))
+        wanted_ref[0:1, at] = sign * lefts + (size >> 3)
+        pick = lax.broadcasted_iota(jnp.int32, (columns, piece), 0) == column
+        pick_ref[:, at] = jnp.where(pick, 1.0, 0.0).astype(jnp.bfloat16)
+
     step = math.gcd(stations, 2 * lane)
-    blocks = stations // step
     sub = lax.broadcasted_iota(jnp.int32, (8, step), 0)
-
-    @pl.loop(0, bins * blocks)
-    def _(item):
-        f = item // blocks
-        at = pl.ds(pl.multiple_of(lax.rem(item, blocks) * step, step), step)
-        number = first + f
-        east = jnp.broadcast_to(coords_ref[0:1, at], (8, step)) * number
-        north = jnp.broadcast_to(coords_ref[1:2, at], (8, step)) * number
-        factor_ref[f, :, at] = jnp.concatenate(cos_sin(east * (8 * sub + 4)), 0).astype(jnp.bfloat16)
-        twice = 2 * cos_sin(16 * north)[0]
-        c2, s2 = cos_sin(2 * east)
-        start = [cos_sin(east + north * (2 * sub + odd)) for odd in (1 - 2 * grid_half, 17 - 2 * grid_half)]
-        turned = [(c * c2 - s * s2, s * c2 + c * s2) for c, s in start]
-        for d, (one, two) in enumerate((start, turned)):
-            for i in range(0, 2 * grid_half, 16):
-                for part in range(2):
-                    rows = pl.ds((2 * part + d) * 2 * grid_half + i, 16)
-                    right_ref[f, rows, at] = jnp.concatenate([one[part], two[part]], 0).astype(jnp.bfloat16)
-                one = tuple(twice * b - a for a, b in zip(one, two))
-                two = tuple(twice * b - a for a, b in zip(two, one))
-
-
-def tables(coords, bins, groups, bins_dev, width):
+    odd = (sub & 1) == 1
+
+    @pl.loop(0, stations // step)
+    def _(block):
+        at = pl.ds(pl.multiple_of(block * step, step), step)
+        east = jnp.broadcast_to(coords_ref[0:1, at], (8, step))
+        north = jnp.broadcast_to(coords_ref[1:2, at], (8, step))
+        for i in range(0, 2 * bins, 8):
+            index = jnp.where(odd, 2 * east, 16 * north) * (first + i // 2 + (sub >> 1))
+            for part, values in enumerate(cos_sin(index)):
+                rows_ref[part, pl.ds(i, 8), :] = values
+        start_unit = east + north * (2 * sub + (1 - 2 * grid_half))
+        factor_unit = east * (8 * sub + 4)
+        start, factor = cos_sin(start_unit * first), cos_sin(factor_unit * first)
+        if bins > 1:
+            start_unit, factor_unit = cos_sin(start_unit), cos_sin(factor_unit)
+        for f in range(bins):
+            if f > 0:
+                start, factor = rotate(start, start_unit), rotate(factor, factor_unit)
+            sixteen, two_east = (
+                tuple(jnp.broadcast_to(rows_ref[part, r:r + 1, :], (8, step)) for part in range(2))
+                for r in (2 * f, 2 * f + 1)
+            )
+            factor_ref[f, :, at] = jnp.concatenate(factor, 0)
+            twice = 2 * sixteen[0]
+            second = rotate(start, sixteen)
+            for d, (one, two) in enumerate(((start, second), (rotate(start, two_east), rotate(second, two_east)))):
+                for i in range(0, 2 * grid_half, 16):
+                    for part in range(2):
+                        rows = pl.ds((2 * part + d) * 2 * grid_half + i, 16)
+                        right_ref[f, rows, at] = jnp.concatenate([one[part], two[part]], 0).astype(jnp.bfloat16)
+                    one = tuple(twice * b - a for a, b in zip(one, two))
+                    two = tuple(twice * b - a for a, b in zip(two, one))
+
+
+def tables(coords, slowness, bins, groups, bins_dev, width):
     stations = coords.shape[1]
     vmem = pl.BlockSpec(memory_space=pltpu.VMEM)
     return pl.pallas_call(
         lambda *refs: tables_kernel(groups, *refs),
         out_shape=(
             jax.ShapeDtypeStruct((bins, 8 * grid_half, stations), jnp.bfloat16),
-            jax.ShapeDtypeStruct((bins, 2 * lefts, stations), jnp.bfloat16),
+            jax.ShapeDtypeStruct((bins, 2 * lefts, stations), jnp.float32),
             jax.ShapeDtypeStruct((2, bins_dev, width), jnp.float32),
+            jax.ShapeDtypeStruct((4 * grid_half, slowness.shape[1]), jnp.bfloat16),
+            jax.ShapeDtypeStruct((1, slowness.shape[1]), jnp.int32),
         ),
-        in_specs=[vmem],
-        out_specs=(vmem,) * 3,
+        in_specs=[vmem] * 2,
+        out_specs=(vmem,) * 5,
+        scratch_shapes=[pltpu.VMEM((2, 8 * pl.cdiv(bins, 4), math.gcd(stations, 2 * lane)), jnp.float32)],
         compiler_params=pltpu.CompilerParams(vmem_limit_bytes=vmem_limit),
         cost_estimate=pl.CostEstimate(flops=bins * stations * 4096, bytes_accessed=bins * stations * 576, transcendentals=0),
         name="tables",
-    )(coords)
+    )(coords, slowness)
 
 
 def whiten_kernel(total_bins, spectra_ref, turn_ref, *refs):
@@ -164,7 +197,7 @@
     )(spectra, turn, *partial)
 
 
-def grid_kernel(white_ref, right_ref, factor_ref, slow_ref, out_ref, left, power):
+def grid_kernel(white_ref, right_ref, factor_ref, pick_ref, wanted_ref, out_ref, left, power):
     sources, bins, rows, width = white_ref.shape
     segs = rows // 2
     basis = 2 * lefts
@@ -176,10 +209,10 @@
         for t in range(width // step):
             at = pl.ds(src * width + t * step, step)
             white = white_ref[src, f, :, pl.ds(t * step, step)].astype(jnp.float32)
-            factor = factor_ref[f, :, at]
+            factor = factor_ref[f, :, at].astype(jnp.float32)
             for r in range(rows):
-                value = jnp.broadcast_to(white[r:r + 1], (basis, step)).astype(jnp.bfloat16)
-                left[f, pl.ds(basis * r, basis), at] = factor * value
+                value = jnp.broadcast_to(white[r:r + 1], (basis, step))
+                left[f, pl.ds(basis * r, basis), at] = (factor * value).astype(jnp.bfloat16)
 
     def finish(f, total):
         found = [0.0] * 4
@@ -198,6 +231,8 @@
         for q in range(4):
             power[pl.ds((4 * f + q) * lefts, lefts), :] = found[q] * norm
 
+    dests, _, beams = out_ref.shape
+
     for f in range(0, bins, 2):
         both = range(f, min(f + 2, bins))
         totals = [0.0] * len(both)
@@ -216,37 +251,25 @@
     high = values.astype(jnp.bfloat16)
     low = (values - high.astype(jnp.float32)).astype(jnp.bfloat16)
     pair = jnp.concatenate([high, low], 1)
-    dests, _, beams = out_ref.shape
     for d in range(dests):
         at = pl.ds(d * beams, beams)
-        east = 2 * slow_ref[0:1, at] + 1
-        north = slow_ref[1:2, at]
-        size = jnp.abs(east)
-        place = (size & 7) >> 1
-        positive = east > 0
-        same = positive == (place >= 2)
-        column = jnp.where(same, north + grid_half, grid_half - 1 - north)
-        column += jnp.where((place == 1) | (place == 2), 0, 2 * grid_half)
-        sign = jnp.where(place >= 2, jnp.where(positive, 0, 1), jnp.where(positive, 2, 3))
-        wanted = sign * lefts + (size >> 3)
-        pick = lax.broadcasted_iota(jnp.int32, (columns, beams), 0) == column
-        pick = jnp.where(pick, 1.0, 0.0).astype(jnp.bfloat16)
+        pick = pick_ref[:, at]
         found = jnp.dot(pair, jnp.concatenate([pick, pick], 0), preferred_element_type=jnp.float32)
-        row = lax.broadcasted_iota(jnp.int32, (4 * lefts, beams), 0) == wanted
+        row = lax.broadcasted_iota(jnp.int32, (4 * lefts, beams), 0) == wanted_ref[0:1, at]
         for f in range(bins):
             part = jnp.where(row, found[f * 4 * lefts:(f + 1) * 4 * lefts], 0.0)
             out_ref[d, pl.ds(f, 1), :] = jnp.sum(part, axis=0, keepdims=True)
 
 
-def beam_grid(white, right, factor, slowness, dests):
+def beam_grid(white, right, factor, pick, wanted, dests):
     sources, bins, rows, width = white.shape
     stations = sources * width
-    beams = slowness.shape[1] // dests
+    beams = pick.shape[1] // dests
     vmem = pl.BlockSpec(memory_space=pltpu.VMEM)
     return pl.pallas_call(
         grid_kernel,
         out_shape=jax.ShapeDtypeStruct((dests, bins, beams), jnp.float32),
-        in_specs=[vmem] * 4,
+        in_specs=[vmem] * 5,
         out_specs=vmem,
         scratch_shapes=[
             pltpu.VMEM((bins, 2 * lefts * rows, stations), jnp.bfloat16),
@@ -255,7 +278,7 @@
         compiler_params=pltpu.CompilerParams(vmem_limit_bytes=vmem_limit),
         cost_estimate=pl.CostEstimate(flops=bins * stations * 4096, bytes_accessed=bins * stations * 576, transcendentals=0),
         name="beam_grid",
-    )(white, right, factor, slowness)
+    )(white, right, factor, pick, wanted)
 
 
 def local(spectra, coords, slowness):
@@ -269,12 +292,12 @@
     partial = [local_sq]
     for shift in range(1, rows):
         partial.append(lax.ppermute(local_sq, "bins", [(i, (i + shift) % rows) for i in range(rows)]))
-    right, factor, turn = tables(coords, bins_own, groups, bins_dev, width)
+    right, factor, turn, pick, wanted = tables(coords, slowness, bins_own, groups, bins_dev, width)
     parts = whiten(spectra, turn, partial, bins_dev * rows, groups)
     if copies > 1:
         parts = jnp.repeat(parts, copies, axis=0)
     white = lax.all_to_all(parts, "sta", 0, 0, tiled=True)
-    powers = beam_grid(white, right, factor, slowness, peers)
+    powers = beam_grid(white, right, factor, pick, wanted, peers)
     powers = lax.all_to_all(powers, "sta", 0, 0, tiled=True)
     return powers[::copies].reshape(bins_dev, -1)
 

time: 36 us -> 34.5 us (0.958)
  blocking collectives: 26.1 us -> 24.6 us
  Pallas kernels: 5.64 us -> 4.17 us
  waiting for transfers between devices: 0.14 us -> 1.58 us
    ppermute x3, waiting for transfers between devices: 0.14 us -> 1.58 us  [local(): lax.ppermute(local_sq, 'bins', [(i, (i + shift) % rows) for i in range(ro...]
    pallas_call x1, Pallas kernels: 2.79 us -> 1.36 us  [tables(): pl.pallas_call(lambda *refs: tables_kernel(groups, *refs), out_shape=(jax...]
    all_to_all x1, blocking collectives: 15.9 us -> 14.5 us  [local(): white = lax.all_to_all(parts, 'sta', 0, 0, tiled=True)]
  transfers between devices with their start and end apart: 3 -> 3, of which waited for: 2 -> 2; matrix products, arithmetic and copies ran while one was open for 0% -> 0% of each run, Pallas kernels for 8% -> 4%
where the time goes in v5:
time: 34.5 us; the launch traced here: 34.3 us
  blocking collectives  24.6 us (71%)
  Pallas kernels  4.17 us (12%)
  starting transfers between devices  3.25 us (9%)
  waiting for transfers between devices  1.58 us (5%)
  local copies, waits for them, and re-layouts  0.63 us (2%)
    all_to_all x1, blocking collectives, local(): white = lax.all_to_all(parts, 'sta', 0, 0, tiled=True)  14.5 us
    all_to_all x1, blocking collectives, local(): powers = lax.all_to_all(powers, 'sta', 0, 0, tiled=True)  10.1 us
    ppermute x3, starting transfers between devices, local(): lax.ppermute(local_sq, 'bins', [(i, (i + shift) % rows) for i in range(ro...  3.25 us
    pallas_call x1, Pallas kernels, beam_grid(): pl.pallas_call(grid_kernel, out_shape=jax.ShapeDtypeStruct((dests, bins,...  1.68 us
    ppermute x3, waiting for transfers between devices, local(): lax.ppermute(local_sq, 'bins', [(i, (i + shift) % rows) for i in range(ro...  1.58 us
    pallas_call x1, Pallas kernels, tables(): pl.pallas_call(lambda *refs: tables_kernel(groups, *refs), out_shape=(jax...  1.36 us
    pallas_call x1, Pallas kernels, sums(): pl.pallas_call(sums_kernel, out_shape=(jax.ShapeDtypeStruct(spectra.shape...  1.02 us
  transfers between devices with their start and end apart: 3, of which 2 were waited for; matrix products, arithmetic and copies ran while one was open for 0% of the time, Pallas kernels for 4%

profile of v5, /device:TPU:0, one launch (start us, length us, event | category | flops | bytes accessed | tf_op | source)
XLA Modules:
  0.0 34.3 jit_solution(11396823847102167669)
XLA Ops:
  0.0 1.0 %sums.1 = (f32[8,256]{1,0:T(8,128)S(1)}, bf16[2,32,8,256]{3,2,1,0:T(8,128)(2,1)S(1)}, s32[2,2048]{1,0:T(2,128)S(1)}, s32[2,2048]{1,0:T(2,128)S(1)}) custom-call(bf16[2,32,8,256]{3,2,1,0:T(8,128)(2,1)} %spectra_hbm.1, s32[2,2048]{1,0:T(2,128)} %coords_hbm.1, s32[2,2048]{1,0:T(2,128)} %slow_hbm.1), custom_call_target="tpu_custom_call" | custom-call | flops 262144 | bytes 262144 | tf_op jit(solution)/shard_map/sums/pallas_call | solution.py:62
  1.0 2.5 %collective-permute-start.2 = (f32[8,256]{1,0:T(8,128)S(1)}, f32[8,256]{1,0:T(8,128)S(1)}, u32[]{:S(2)}, u32[]{:S(2)}) collective-permute-start(f32[8,256]{1,0:T(8,128)S(1)} %get-tuple-element.18.refs_2_), channel_id=1, source_target_pairs={{0,24},{8,0},{16,8},{24,16},{1,25},{9,1},{17,9},{25,17},{2,26},{10... | collective-permute-start | bytes 24584 | tf_op jit(solution)/shard_map/ppermute | solution.py:294
  3.5 0.6 %collective-permute-start.1 = (f32[8,256]{1,0:T(8,128)S(1)}, f32[8,256]{1,0:T(8,128)S(1)}, u32[]{:S(2)}, u32[]{:S(2)}) collective-permute-start(f32[8,256]{1,0:T(8,128)S(1)} %get-tuple-element.18.refs_2_), channel_id=1, source_target_pairs={{0,16},{8,24},{16,0},{24,8},{1,17},{9,25},{17,1},{25,9},{2,18},{10... | collective-permute-start | bytes 24584 | tf_op jit(solution)/shard_map/ppermute | solution.py:294
  4.1 0.2 collective-permute-start
  4.3 1.4 %tables.1 = (bf16[4,256,2048]{2,1,0:T(8,128)(2,1)S(1)}, f32[4,16,2048]{2,1,0:T(8,128)S(1)}, f32[2,32,256]{2,1,0:T(8,128)S(1)}, bf16[128,2048]{1,0:T(8,128)(2,1)S(1)}, s32[1,2048]{1,0:T(1,128)S(1)}) custom-call(s32[2,2048]{1,0:T(2,128)S(1)} %get-tuple-element.15.refs_0_, s32[2,2048]{1,0:T(2,128)S(1)} %get-tuple-element.16.refs_1_), custom_call_target="tpu_custom_call" | custom-call | flops 33554432 | bytes 4718592 | tf_op jit(solution)/shard_map/tables/pallas_call | solution.py:155
  5.6 0.0 collective-permute-done.2.refs_5_
  5.6 1.5 %collective-permute-done.1.refs_4_ = f32[8,256]{1,0:T(8,128)S(1)} collective-permute-done((f32[8,256]{1,0:T(8,128)S(1)}, f32[8,256]{1,0:T(8,128)S(1)}, u32[]{:S(2)}, u32[]{:S(2)}) %collective-permute-start.1) | collective-permute-done | bytes 8224 | tf_op jit(solution)/shard_map/ppermute | solution.py:294
  7.2 0.1 collective-permute-done.refs_3_
  7.2 0.1 whiten.1
  7.3 14.5 %all_to_all.10.white_ref = bf16[8,4,16,256]{3,2,1,0:T(8,128)(2,1)S(1)} all-to-all(bf16[8,4,16,256]{3,2,1,0:T(8,128)(2,1)S(1)} %whiten.1), channel_id=1, replica_groups=mesh['bins'=4,'sta'=8] {'sta'}, dimensions={0} | all-to-all | bytes 524288 | tf_op jit(solution)/shard_map/all_to_all | solution.py:299
  21.9 1.7 %beam_grid.1 = f32[8,4,256]{2,1,0:T(4,128)S(1)} custom-call(bf16[8,4,16,256]{3,2,1,0:T(8,128)(2,1)S(1)} %all_to_all.10.white_ref, bf16[4,256,2048]{2,1,0:T(8,128)(2,1)S(1)} %get-tuple-element.19.right_ref, f32[4,16,2048]{2,1,0:T(8,128)S(1)} %get-tuple-element.20.factor_ref, bf16[128,2048]{1,0:T(8,128)(2,1)S(1)} %get-tuple-element.21.pick_ref, ...), custom_call_target="tpu_custom_call" | custom-call | flops 33554432 | bytes 4718592 | tf_op jit(solution)/shard_map/beam_grid/pallas_call | solution.py:269
  23.6 10.1 %all_to_all.11 = f32[8,4,256]{2,1,0:T(4,128)S(1)} all-to-all(f32[8,4,256]{2,1,0:T(4,128)S(1)} %beam_grid.1), channel_id=1, replica_groups=mesh['bins'=4,'sta'=8] {'sta'}, dimensions={0} | all-to-all | bytes 65536 | tf_op jit(solution)/shard_map/all_to_all | solution.py:301
  33.6 0.6 %reshape.3 = f32[32,256]{1,0:T(8,128)} reshape(f32[8,4,256]{2,1,0:T(4,128)S(1)} %all_to_all.11) | data formatting | bytes 65536 | tf_op jit(solution)/shard_map/reshape | solution.py:302
Async XLA Ops:
  1.0 4.6 %collective-permute-start.2 = (f32[8,256]{1,0:T(8,128)S(1)}, f32[8,256]{1,0:T(8,128)S(1)}, u32[]{:S(2)}, u32[]{:S(2)}) collective-permute-start(f32[8,256]{1,0:T(8,128)S(1)} %get-tuple-element.18.refs_2_), channel_id=1, source_target_pairs={{0,24},{8,0},{16,8},{24,16},{1,25},{9,1},{17,9},{25,17},{2,26},{10... | collective-permute-start | bytes 24584 | tf_op jit(solution)/shard_map/ppermute | solution.py:294
  3.5 3.7 %collective-permute-start.1 = (f32[8,256]{1,0:T(8,128)S(1)}, f32[8,256]{1,0:T(8,128)S(1)}, u32[]{:S(2)}, u32[]{:S(2)}) collective-permute-start(f32[8,256]{1,0:T(8,128)S(1)} %get-tuple-element.18.refs_2_), channel_id=1, source_target_pairs={{0,16},{8,24},{16,0},{24,8},{1,17},{9,25},{17,1},{25,9},{2,18},{10... | collective-permute-start | bytes 24584 | tf_op jit(solution)/shard_map/ppermute | solution.py:294
  4.1 3.1 %collective-permute-start = (f32[8,256]{1,0:T(8,128)S(1)}, f32[8,256]{1,0:T(8,128)S(1)}, u32[]{:S(2)}, u32[]{:S(2)}) collective-permute-start(f32[8,256]{1,0:T(8,128)S(1)} %get-tuple-element.18.refs_2_), channel_id=1, source_target_pairs={{0,8},{8,16},{16,24},{24,0},{1,9},{9,17},{17,25},{25,1},{2,10},{10... | collective-permute-start | bytes 24584 | tf_op jit(solution)/shard_map/ppermute | solution.py:294
